TPU v7x, 128 devices: a whole 4x4x4 slice. The times are simulated.
128 devices in a mesh: data: 1, time: 128 (over z, y, x, core).
Axes of the slice: x: 4, y: 4, z: 4, core: 2. Of those that a mesh axis runs over, the one named last changes fastest.
Arguments:
- x_init: float32 [64, 16, 10], P('data')
- w_in: bfloat16 [10, 256], replicated
- w_out: bfloat16 [256, 10], replicated
- mod_scale: bfloat16 [2048, 256], P('time')
- mod_shift: bfloat16 [2048, 256], P('time')
- step_size: float32 [2048], P('time')
Outputs:
- output: float32 [2048, 64, 16, 10], P('time', 'data')
All inputs are finite; a program needn't handle non-finite values.
Results may differ from a plain program's by a relative error of at most 0.001.
Values are sent between devices in bfloat16 or wider.
A program may use at most 1 GiB of HBM per device.

v0:
```python
import jax
import jax.numpy as jnp
from jax import lax
from jax.sharding import PartitionSpec as P

SWEEPS = 4


def drift_block(pre_act, scale, shift, w_out):
    hidden_act = jax.nn.gelu(pre_act * scale + shift, approximate=True)
    return jnp.einsum("kbnd,dc->kbnc", hidden_act.astype(jnp.bfloat16), w_out, preferred_element_type=jnp.float32)


def solution(mesh):
    n_time = mesh.shape["time"]
    from_next = [(source, source - 1) for source in range(1, n_time)]
    hop_dists = [2 ** power for power in range(n_time) if 2 ** power < n_time]

    def local(x_init, w_in, w_out, mod_scale, mod_shift, step_size):
        scale = (1.0 + mod_scale.astype(jnp.float32))[:, None, None, :]
        shift = mod_shift.astype(jnp.float32)[:, None, None, :]
        pre_act = jnp.einsum("bnc,cd->bnd", x_init.astype(jnp.bfloat16), w_in, preferred_element_type=jnp.float32)[None]
        latents = None
        for sweep in range(SWEEPS):
            if sweep > 0:
                pre_act = jnp.einsum("kbnc,cd->kbnd", latents.astype(jnp.bfloat16), w_in, preferred_element_type=jnp.float32)
            drifts = drift_block(pre_act, scale, shift, w_out)
            next_first = lax.ppermute(drifts[0], "time", from_next)
            next_drifts = jnp.concatenate([drifts[1:], next_first[None]], axis=0)
            increments = step_size[:, None, None, None] * (0.5 * (drifts + next_drifts))
            local_cum = jnp.cumsum(increments, axis=0)
            local_excl = jnp.concatenate([jnp.zeros_like(local_cum[:1]), local_cum[:-1]], axis=0)
            dev_total = local_cum[-1]
            inclusive = dev_total
            for distance in hop_dists:
                inclusive = inclusive + lax.ppermute(inclusive, "time", [(source, source + distance) for source in range(n_time - distance)])
            offset = inclusive - dev_total
            latents = x_init[None] + (offset[None] + local_excl)
        return latents

    return jax.shard_map(local, mesh=mesh, in_specs=(P("data"), P(), P(), P("time"), P("time"), P("time")), out_specs=P("time", "data"), check_vma=False)
```

profile of v0, /device:TPU:0, one launch (start us, length us, event | category | flops | bytes accessed | tf_op | source)
XLA Modules:
  0.0 570.3 jit_solution(14895802219891923169)
XLA Ops:
  2.9 7.0 %fusion.32 = f32[16,64,16,10]{3,2,1,0:T(8,128)S(1)} fusion(f32[16,256]{1,0:T(8,128)S(1)} %convert_element_type.32, f32[16,256]{1,0:T(8,128)S(1)} %convert_add_fusion, f32[64,16,256]{2,1,0:T(8,128)S(1)} %fusion.84, bf16[256,10]{0,1:T(8,128)(2,1)} %param.8), kind=kOutput, calls=%fused_computation.36 | convolution fusion | flops 130023424 | bytes 1741824 | tf_op jit(solution)/shard_map/kbnd,dc->kbnc/dot_general | solution.py:11
  14.6 6.2 %fusion.35 = f32[16,64,16,10]{3,2,1,0:T(8,128)} fusion(f32[16,64,16,10]{3,2,1,0:T(8,128)} %copy-done.3, f32[1,64,16,10]{3,2,1,0:T(8,128)} %bitcast.65, f32[15,64,16,10]{3,2,1,0:T(8,128)S(1)} %slice.64, f32[16]{0:T(128)S(1)} %broadcast_multiply_fusion), kind=kOutput, calls=%fused_computation.39 | output fusion | flops 2949120 | bytes 1966144 | tf_op jit(solution)/shard_map/jit(cumsum)/reduce_window_sum | solution.py:31
  21.9 8.7 %collective-permute-start.1 = (f32[64,16,10]{2,1,0:T(8,128)S(1)}, f32[64,16,10]{2,1,0:T(8,128)S(1)}, u32[]{:S(2)}, u32[]{:S(2)}) collective-permute-start(f32[64,16,10]{2,1,0:T(8,128)S(1)} %slice_bitcast_fusion.6), channel_id=1, source_target_pairs={{0,1},{1,2},{2,3},{3,4},{4,5},{5,6},{6,7},{7,8},{8,9},{9,10},{10,1... | collective-permute-start | bytes 122888 | tf_op jit(solution)/shard_map/ppermute | solution.py:36
  33.1 8.9 %collective-permute-start.2 = (f32[64,16,10]{2,1,0:T(8,128)S(1)}, f32[64,16,10]{2,1,0:T(8,128)S(1)}, u32[]{:S(2)}, u32[]{:S(2)}) collective-permute-start(f32[64,16,10]{2,1,0:T(8,128)S(1)} %fusion.112), channel_id=1, source_target_pairs={{0,2},{1,3},{2,4},{3,5},{4,6},{5,7},{6,8},{7,9},{8,10},{9,11},{10,... | collective-permute-start | bytes 122888 | tf_op jit(solution)/shard_map/ppermute | solution.py:36
  42.0 10.4 %collective-permute-done.2 = f32[64,16,10]{2,1,0:T(8,128)S(1)} collective-permute-done((f32[64,16,10]{2,1,0:T(8,128)S(1)}, f32[64,16,10]{2,1,0:T(8,128)S(1)}, u32[]{:S(2)}, u32[]{:S(2)}) %collective-permute-start.2) | collective-permute-done | bytes 40992 | tf_op jit(solution)/shard_map/ppermute | solution.py:36
  52.5 6.8 %collective-permute-start.3 = (f32[64,16,10]{2,1,0:T(8,128)S(1)}, f32[64,16,10]{2,1,0:T(8,128)S(1)}, u32[]{:S(2)}, u32[]{:S(2)}) collective-permute-start(f32[64,16,10]{2,1,0:T(8,128)S(1)} %add.227), channel_id=1, source_target_pairs={{0,4},{1,5},{2,6},{3,7},{4,8},{5,9},{6,10},{7,11},{8,12},{9,13},{1... | collective-permute-start | bytes 122888 | tf_op jit(solution)/shard_map/ppermute | solution.py:36
  59.3 11.6 %collective-permute-done.3 = f32[64,16,10]{2,1,0:T(8,128)S(1)} collective-permute-done((f32[64,16,10]{2,1,0:T(8,128)S(1)}, f32[64,16,10]{2,1,0:T(8,128)S(1)}, u32[]{:S(2)}, u32[]{:S(2)}) %collective-permute-start.3) | collective-permute-done | bytes 40992 | tf_op jit(solution)/shard_map/ppermute | solution.py:36
  75.6 9.0 %collective-permute-done.4 = f32[64,16,10]{2,1,0:T(8,128)S(1)} collective-permute-done((f32[64,16,10]{2,1,0:T(8,128)S(1)}, f32[64,16,10]{2,1,0:T(8,128)S(1)}, u32[]{:S(2)}, u32[]{:S(2)}) %collective-permute-start.4) | collective-permute-done | bytes 40992 | tf_op jit(solution)/shard_map/ppermute | solution.py:36
  90.8 8.5 %collective-permute-done.5 = f32[64,16,10]{2,1,0:T(8,128)S(1)} collective-permute-done((f32[64,16,10]{2,1,0:T(8,128)S(1)}, f32[64,16,10]{2,1,0:T(8,128)S(1)}, u32[]{:S(2)}, u32[]{:S(2)}) %collective-permute-start.5) | collective-permute-done | bytes 40992 | tf_op jit(solution)/shard_map/ppermute | solution.py:36
  99.3 15.5 %collective-permute-start.6 = (f32[64,16,10]{2,1,0:T(8,128)S(1)}, f32[64,16,10]{2,1,0:T(8,128)S(1)}, u32[]{:S(2)}, u32[]{:S(2)}) collective-permute-start(f32[64,16,10]{2,1,0:T(8,128)S(1)} %add.230), channel_id=1, source_target_pairs={{0,32},{1,33},{2,34},{3,35},{4,36},{5,37},{6,38},{7,39},{8,40},{9,... | collective-permute-start | bytes 122888 | tf_op jit(solution)/shard_map/ppermute | solution.py:36
  114.8 10.8 %collective-permute-done.6 = f32[64,16,10]{2,1,0:T(8,128)S(1)} collective-permute-done((f32[64,16,10]{2,1,0:T(8,128)S(1)}, f32[64,16,10]{2,1,0:T(8,128)S(1)}, u32[]{:S(2)}, u32[]{:S(2)}) %collective-permute-start.6) | collective-permute-done | bytes 40992 | tf_op jit(solution)/shard_map/ppermute | solution.py:36
  125.7 8.0 %collective-permute-start.7 = (f32[64,16,10]{2,1,0:T(8,128)S(1)}, f32[64,16,10]{2,1,0:T(8,128)S(1)}, u32[]{:S(2)}, u32[]{:S(2)}) collective-permute-start(f32[64,16,10]{2,1,0:T(8,128)S(1)} %add.231), channel_id=1, source_target_pairs={{0,64},{1,65},{2,66},{3,67},{4,68},{5,69},{6,70},{7,71},{8,72},{9,... | collective-permute-start | bytes 122888 | tf_op jit(solution)/shard_map/ppermute | solution.py:36
  134.1 7.2 %slice.67 = f32[15,64,16,10]{3,2,1,0:T(8,128)} slice(f32[16,64,16,10]{3,2,1,0:T(8,128)} %fusion.35), slice={[0:15], [0:64], [0:16], [0:10]} | slice | bytes 1228800 | tf_op jit(solution)/shard_map/slice | solution.py:32
  142.5 12.0 %fusion.73 = f32[16,64,16,10]{3,2,1,0:T(8,128)} fusion(f32[16,256]{1,0:T(8,128)S(1)} %convert_element_type.32, f32[16,256]{1,0:T(8,128)S(1)} %convert_add_fusion, f32[15,64,16,10]{3,2,1,0:T(8,128)} %slice.67, f32[64,16,10]{2,1,0:T(8,128)S(1)} %add_subtract_fusion.3, f32[64,16,10]{2,1,0:T(8,128)S(1)} %copy.25, bf16[10,256]{1,0:T(8,128)(2,1)S(1)} %copy-done, ...), kind=kOutput, calls=%fused_computation.80 | convolution fusion | flops 214401024 | bytes 1394688 | tf_op jit(solution)/shard_map/kbnd,dc->kbnc/dot_general | solution.py:11
  159.8 6.2 %fusion.40 = f32[16,64,16,10]{3,2,1,0:T(8,128)} fusion(f32[16,64,16,10]{3,2,1,0:T(8,128)} %fusion.73, f32[1,64,16,10]{3,2,1,0:T(8,128)} %bitcast.9, f32[15,64,16,10]{3,2,1,0:T(8,128)S(1)} %slice-done.4, f32[16]{0:T(128)S(1)} %broadcast_multiply_fusion), kind=kOutput, calls=%fused_computation.44 | output fusion | flops 2949120 | bytes 1966144 | tf_op jit(solution)/shard_map/jit(cumsum)/reduce_window_sum | solution.py:31
  172.2 8.9 %collective-permute-start.10 = (f32[64,16,10]{2,1,0:T(8,128)S(1)}, f32[64,16,10]{2,1,0:T(8,128)S(1)}, u32[]{:S(2)}, u32[]{:S(2)}) collective-permute-start(f32[64,16,10]{2,1,0:T(8,128)S(1)} %fusion.113), channel_id=1, source_target_pairs={{0,2},{1,3},{2,4},{3,5},{4,6},{5,7},{6,8},{7,9},{8,10},{9,11},{10,... | collective-permute-start | bytes 122888 | tf_op jit(solution)/shard_map/ppermute | solution.py:36
  181.1 8.6 %collective-permute-done.10 = f32[64,16,10]{2,1,0:T(8,128)S(1)} collective-permute-done((f32[64,16,10]{2,1,0:T(8,128)S(1)}, f32[64,16,10]{2,1,0:T(8,128)S(1)}, u32[]{:S(2)}, u32[]{:S(2)}) %collective-permute-start.10) | collective-permute-done | bytes 40992 | tf_op jit(solution)/shard_map/ppermute | solution.py:36
  195.1 12.2 %collective-permute-done.11 = f32[64,16,10]{2,1,0:T(8,128)S(1)} collective-permute-done((f32[64,16,10]{2,1,0:T(8,128)S(1)}, f32[64,16,10]{2,1,0:T(8,128)S(1)}, u32[]{:S(2)}, u32[]{:S(2)}) %collective-permute-start.11) | collective-permute-done | bytes 40992 | tf_op jit(solution)/shard_map/ppermute | solution.py:36
  211.9 10.4 %collective-permute-done.12 = f32[64,16,10]{2,1,0:T(8,128)S(1)} collective-permute-done((f32[64,16,10]{2,1,0:T(8,128)S(1)}, f32[64,16,10]{2,1,0:T(8,128)S(1)}, u32[]{:S(2)}, u32[]{:S(2)}) %collective-permute-start.12) | collective-permute-done | bytes 40992 | tf_op jit(solution)/shard_map/ppermute | solution.py:36
  224.3 7.7 %collective-permute-done.13 = f32[64,16,10]{2,1,0:T(8,128)S(1)} collective-permute-done((f32[64,16,10]{2,1,0:T(8,128)S(1)}, f32[64,16,10]{2,1,0:T(8,128)S(1)}, u32[]{:S(2)}, u32[]{:S(2)}) %collective-permute-start.13) | collective-permute-done | bytes 40992 | tf_op jit(solution)/shard_map/ppermute | solution.py:36
  232.0 19.0 %collective-permute-start.14 = (f32[64,16,10]{2,1,0:T(8,128)S(1)}, f32[64,16,10]{2,1,0:T(8,128)S(1)}, u32[]{:S(2)}, u32[]{:S(2)}) collective-permute-start(f32[64,16,10]{2,1,0:T(8,128)S(1)} %add.244), channel_id=1, source_target_pairs={{0,32},{1,33},{2,34},{3,35},{4,36},{5,37},{6,38},{7,39},{8,40},{9,... | collective-permute-start | bytes 122888 | tf_op jit(solution)/shard_map/ppermute | solution.py:36
  251.0 6.6 %collective-permute-done.14 = f32[64,16,10]{2,1,0:T(8,128)S(1)} collective-permute-done((f32[64,16,10]{2,1,0:T(8,128)S(1)}, f32[64,16,10]{2,1,0:T(8,128)S(1)}, u32[]{:S(2)}, u32[]{:S(2)}) %collective-permute-start.14) | collective-permute-done | bytes 40992 | tf_op jit(solution)/shard_map/ppermute | solution.py:36
  257.7 16.2 %collective-permute-start.15 = (f32[64,16,10]{2,1,0:T(8,128)S(1)}, f32[64,16,10]{2,1,0:T(8,128)S(1)}, u32[]{:S(2)}, u32[]{:S(2)}) collective-permute-start(f32[64,16,10]{2,1,0:T(8,128)S(1)} %add.245), channel_id=1, source_target_pairs={{0,64},{1,65},{2,66},{3,67},{4,68},{5,69},{6,70},{7,71},{8,72},{9,... | collective-permute-start | bytes 122888 | tf_op jit(solution)/shard_map/ppermute | solution.py:36
  280.7 12.0 %fusion.72 = f32[16,64,16,10]{3,2,1,0:T(8,128)} fusion(f32[16,256]{1,0:T(8,128)S(1)} %convert_element_type.32, f32[16,256]{1,0:T(8,128)S(1)} %convert_add_fusion, f32[15,64,16,10]{3,2,1,0:T(8,128)} %slice.71, f32[64,16,10]{2,1,0:T(8,128)S(1)} %add_subtract_fusion.2, f32[64,16,10]{2,1,0:T(8,128)S(1)} %copy-done.5, bf16[10,256]{1,0:T(8,128)(2,1)S(1)} %copy-done, ...), kind=kOutput, calls=%fused_computation.79 | convolution fusion | flops 214401024 | bytes 1394688 | tf_op jit(solution)/shard_map/kbnd,dc->kbnc/dot_general | solution.py:11
  298.0 6.2 %fusion.45 = f32[16,64,16,10]{3,2,1,0:T(8,128)} fusion(f32[16,64,16,10]{3,2,1,0:T(8,128)} %fusion.72, f32[1,64,16,10]{3,2,1,0:T(8,128)} %bitcast.12, f32[15,64,16,10]{3,2,1,0:T(8,128)S(1)} %slice-done.5, f32[16]{0:T(128)S(1)} %broadcast_multiply_fusion), kind=kOutput, calls=%fused_computation.49 | output fusion | flops 2949120 | bytes 1966144 | tf_op jit(solution)/shard_map/jit(cumsum)/reduce_window_sum | solution.py:31
  311.1 8.9 %collective-permute-start.18 = (f32[64,16,10]{2,1,0:T(8,128)S(1)}, f32[64,16,10]{2,1,0:T(8,128)S(1)}, u32[]{:S(2)}, u32[]{:S(2)}) collective-permute-start(f32[64,16,10]{2,1,0:T(8,128)S(1)} %fusion.114), channel_id=1, source_target_pairs={{0,2},{1,3},{2,4},{3,5},{4,6},{5,7},{6,8},{7,9},{8,10},{9,11},{10,... | collective-permute-start | bytes 122888 | tf_op jit(solution)/shard_map/ppermute | solution.py:36
  320.0 8.6 %collective-permute-done.18 = f32[64,16,10]{2,1,0:T(8,128)S(1)} collective-permute-done((f32[64,16,10]{2,1,0:T(8,128)S(1)}, f32[64,16,10]{2,1,0:T(8,128)S(1)}, u32[]{:S(2)}, u32[]{:S(2)}) %collective-permute-start.18) | collective-permute-done | bytes 40992 | tf_op jit(solution)/shard_map/ppermute | solution.py:36
  331.2 12.1 %collective-permute-done.19 = f32[64,16,10]{2,1,0:T(8,128)S(1)} collective-permute-done((f32[64,16,10]{2,1,0:T(8,128)S(1)}, f32[64,16,10]{2,1,0:T(8,128)S(1)}, u32[]{:S(2)}, u32[]{:S(2)}) %collective-permute-start.19) | collective-permute-done | bytes 40992 | tf_op jit(solution)/shard_map/ppermute | solution.py:36
  343.4 6.6 %collective-permute-start.20 = (f32[64,16,10]{2,1,0:T(8,128)S(1)}, f32[64,16,10]{2,1,0:T(8,128)S(1)}, u32[]{:S(2)}, u32[]{:S(2)}) collective-permute-start(f32[64,16,10]{2,1,0:T(8,128)S(1)} %add.256), channel_id=1, source_target_pairs={{0,8},{1,9},{2,10},{3,11},{4,12},{5,13},{6,14},{7,15},{8,16},{9,17... | collective-permute-start | bytes 122888 | tf_op jit(solution)/shard_map/ppermute | solution.py:36
  350.1 6.6 %collective-permute-done.20 = f32[64,16,10]{2,1,0:T(8,128)S(1)} collective-permute-done((f32[64,16,10]{2,1,0:T(8,128)S(1)}, f32[64,16,10]{2,1,0:T(8,128)S(1)}, u32[]{:S(2)}, u32[]{:S(2)}) %collective-permute-start.20) | collective-permute-done | bytes 40992 | tf_op jit(solution)/shard_map/ppermute | solution.py:36
  362.6 9.8 %collective-permute-done.21 = f32[64,16,10]{2,1,0:T(8,128)S(1)} collective-permute-done((f32[64,16,10]{2,1,0:T(8,128)S(1)}, f32[64,16,10]{2,1,0:T(8,128)S(1)}, u32[]{:S(2)}, u32[]{:S(2)}) %collective-permute-start.21) | collective-permute-done | bytes 40992 | tf_op jit(solution)/shard_map/ppermute | solution.py:36
  372.4 16.8 %collective-permute-start.22 = (f32[64,16,10]{2,1,0:T(8,128)S(1)}, f32[64,16,10]{2,1,0:T(8,128)S(1)}, u32[]{:S(2)}, u32[]{:S(2)}) collective-permute-start(f32[64,16,10]{2,1,0:T(8,128)S(1)} %add.258), channel_id=1, source_target_pairs={{0,32},{1,33},{2,34},{3,35},{4,36},{5,37},{6,38},{7,39},{8,40},{9,... | collective-permute-start | bytes 122888 | tf_op jit(solution)/shard_map/ppermute | solution.py:36
  389.2 6.6 %collective-permute-done.22 = f32[64,16,10]{2,1,0:T(8,128)S(1)} collective-permute-done((f32[64,16,10]{2,1,0:T(8,128)S(1)}, f32[64,16,10]{2,1,0:T(8,128)S(1)}, u32[]{:S(2)}, u32[]{:S(2)}) %collective-permute-start.22) | collective-permute-done | bytes 40992 | tf_op jit(solution)/shard_map/ppermute | solution.py:36
  395.9 17.4 %collective-permute-start.23 = (f32[64,16,10]{2,1,0:T(8,128)S(1)}, f32[64,16,10]{2,1,0:T(8,128)S(1)}, u32[]{:S(2)}, u32[]{:S(2)}) collective-permute-start(f32[64,16,10]{2,1,0:T(8,128)S(1)} %add.259), channel_id=1, source_target_pairs={{0,64},{1,65},{2,66},{3,67},{4,68},{5,69},{6,70},{7,71},{8,72},{9,... | collective-permute-start | bytes 122888 | tf_op jit(solution)/shard_map/ppermute | solution.py:36
  420.0 12.0 %fusion.71 = f32[16,64,16,10]{3,2,1,0:T(8,128)} fusion(f32[16,256]{1,0:T(8,128)S(1)} %convert_element_type.32, f32[16,256]{1,0:T(8,128)S(1)} %convert_add_fusion, f32[15,64,16,10]{3,2,1,0:T(8,128)} %slice.75, f32[64,16,10]{2,1,0:T(8,128)S(1)} %add_subtract_fusion.1, f32[64,16,10]{2,1,0:T(8,128)S(1)} %copy-done.6, bf16[10,256]{1,0:T(8,128)(2,1)S(1)} %copy-done, ...), kind=kOutput, calls=%fused_computation.78 | convolution fusion | flops 214401024 | bytes 1394688 | tf_op jit(solution)/shard_map/kbnd,dc->kbnc/dot_general | solution.py:11
  437.3 6.2 %fusion.50 = f32[16,64,16,10]{3,2,1,0:T(8,128)} fusion(f32[16,64,16,10]{3,2,1,0:T(8,128)} %fusion.71, f32[1,64,16,10]{3,2,1,0:T(8,128)} %bitcast.15, f32[15,64,16,10]{3,2,1,0:T(8,128)S(1)} %slice-done.3, f32[16]{0:T(128)S(1)} %broadcast_multiply_fusion), kind=kOutput, calls=%fused_computation.54 | output fusion | flops 2949120 | bytes 1966144 | tf_op jit(solution)/shard_map/jit(cumsum)/reduce_window_sum | solution.py:31
  450.0 8.9 %collective-permute-start.26 = (f32[64,16,10]{2,1,0:T(8,128)S(1)}, f32[64,16,10]{2,1,0:T(8,128)S(1)}, u32[]{:S(2)}, u32[]{:S(2)}) collective-permute-start(f32[64,16,10]{2,1,0:T(8,128)S(1)} %fusion.115), channel_id=1, source_target_pairs={{0,2},{1,3},{2,4},{3,5},{4,6},{5,7},{6,8},{7,9},{8,10},{9,11},{10,... | collective-permute-start | bytes 122888 | tf_op jit(solution)/shard_map/ppermute | solution.py:36
  458.9 8.6 %collective-permute-done.26 = f32[64,16,10]{2,1,0:T(8,128)S(1)} collective-permute-done((f32[64,16,10]{2,1,0:T(8,128)S(1)}, f32[64,16,10]{2,1,0:T(8,128)S(1)}, u32[]{:S(2)}, u32[]{:S(2)}) %collective-permute-start.26) | collective-permute-done | bytes 40992 | tf_op jit(solution)/shard_map/ppermute | solution.py:36
  470.1 12.1 %collective-permute-done.27 = f32[64,16,10]{2,1,0:T(8,128)S(1)} collective-permute-done((f32[64,16,10]{2,1,0:T(8,128)S(1)}, f32[64,16,10]{2,1,0:T(8,128)S(1)}, u32[]{:S(2)}, u32[]{:S(2)}) %collective-permute-start.27) | collective-permute-done | bytes 40992 | tf_op jit(solution)/shard_map/ppermute | solution.py:36
  482.3 6.6 %collective-permute-start.28 = (f32[64,16,10]{2,1,0:T(8,128)S(1)}, f32[64,16,10]{2,1,0:T(8,128)S(1)}, u32[]{:S(2)}, u32[]{:S(2)}) collective-permute-start(f32[64,16,10]{2,1,0:T(8,128)S(1)} %add.270), channel_id=1, source_target_pairs={{0,8},{1,9},{2,10},{3,11},{4,12},{5,13},{6,14},{7,15},{8,16},{9,17... | collective-permute-start | bytes 122888 | tf_op jit(solution)/shard_map/ppermute | solution.py:36
  488.9 6.6 %collective-permute-done.28 = f32[64,16,10]{2,1,0:T(8,128)S(1)} collective-permute-done((f32[64,16,10]{2,1,0:T(8,128)S(1)}, f32[64,16,10]{2,1,0:T(8,128)S(1)}, u32[]{:S(2)}, u32[]{:S(2)}) %collective-permute-start.28) | collective-permute-done | bytes 40992 | tf_op jit(solution)/shard_map/ppermute | solution.py:36
  495.6 6.7 %collective-permute-start.29 = (f32[64,16,10]{2,1,0:T(8,128)S(1)}, f32[64,16,10]{2,1,0:T(8,128)S(1)}, u32[]{:S(2)}, u32[]{:S(2)}) collective-permute-start(f32[64,16,10]{2,1,0:T(8,128)S(1)} %add.271), channel_id=1, source_target_pairs={{0,16},{1,17},{2,18},{3,19},{4,20},{5,21},{6,22},{7,23},{8,24},{9,... | collective-permute-start | bytes 122888 | tf_op jit(solution)/shard_map/ppermute | solution.py:36
  502.3 10.8 %collective-permute-done.29 = f32[64,16,10]{2,1,0:T(8,128)S(1)} collective-permute-done((f32[64,16,10]{2,1,0:T(8,128)S(1)}, f32[64,16,10]{2,1,0:T(8,128)S(1)}, u32[]{:S(2)}, u32[]{:S(2)}) %collective-permute-start.29) | collective-permute-done | bytes 40992 | tf_op jit(solution)/shard_map/ppermute | solution.py:36
  513.2 15.2 %collective-permute-start.30 = (f32[64,16,10]{2,1,0:T(8,128)S(1)}, f32[64,16,10]{2,1,0:T(8,128)S(1)}, u32[]{:S(2)}, u32[]{:S(2)}) collective-permute-start(f32[64,16,10]{2,1,0:T(8,128)S(1)} %add.272), channel_id=1, source_target_pairs={{0,32},{1,33},{2,34},{3,35},{4,36},{5,37},{6,38},{7,39},{8,40},{9,... | collective-permute-start | bytes 122888 | tf_op jit(solution)/shard_map/ppermute | solution.py:36
  528.4 6.6 %collective-permute-done.30 = f32[64,16,10]{2,1,0:T(8,128)S(1)} collective-permute-done((f32[64,16,10]{2,1,0:T(8,128)S(1)}, f32[64,16,10]{2,1,0:T(8,128)S(1)}, u32[]{:S(2)}, u32[]{:S(2)}) %collective-permute-start.30) | collective-permute-done | bytes 40992 | tf_op jit(solution)/shard_map/ppermute | solution.py:36
  535.1 17.5 %collective-permute-start.31 = (f32[64,16,10]{2,1,0:T(8,128)S(1)}, f32[64,16,10]{2,1,0:T(8,128)S(1)}, u32[]{:S(2)}, u32[]{:S(2)}) collective-permute-start(f32[64,16,10]{2,1,0:T(8,128)S(1)} %add.273), channel_id=1, source_target_pairs={{0,64},{1,65},{2,66},{3,67},{4,68},{5,69},{6,70},{7,71},{8,72},{9,... | collective-permute-start | bytes 122888 | tf_op jit(solution)/shard_map/ppermute | solution.py:36
  552.6 6.6 %collective-permute-done.31 = f32[64,16,10]{2,1,0:T(8,128)S(1)} collective-permute-done((f32[64,16,10]{2,1,0:T(8,128)S(1)}, f32[64,16,10]{2,1,0:T(8,128)S(1)}, u32[]{:S(2)}, u32[]{:S(2)}) %collective-permute-start.31) | collective-permute-done | bytes 40992 | tf_op jit(solution)/shard_map/ppermute | solution.py:36
  563.6 6.7 %copy.27 = f32[16,64,16,10]{1,2,3,0:T(8,128)} copy(f32[16,64,16,10]{3,2,1,0:T(8,128)} %add_add_fusion) | data formatting | bytes 1310720 | tf_op jit(solution)/shard_map/add | solution.py:38
  (110 shorter events, 100.8 us)
Async XLA Ops:
  2.9 8.4 %copy-start.11 = (f32[16]{0:T(128)S(1)}, f32[16]{0:T(128)}, u32[]{:S(2)}) copy-start(f32[16]{0:T(128)} %param.11) | copy-start | bytes 196
  9.9 3.7 copy-start.3
  10.0 3.8 collective-permute-start
  20.8 113.0 %copy-start.9 = (f32[64,16,10]{0,1,2:T(8,128)S(1)}, f32[64,16,10]{0,1,2:T(8,128)}, u32[]{:S(2)}) copy-start(f32[64,16,10]{0,1,2:T(8,128)} %param.6) | copy-start | bytes 122884
  21.9 10.1 %collective-permute-start.1 = (f32[64,16,10]{2,1,0:T(8,128)S(1)}, f32[64,16,10]{2,1,0:T(8,128)S(1)}, u32[]{:S(2)}, u32[]{:S(2)}) collective-permute-start(f32[64,16,10]{2,1,0:T(8,128)S(1)} %slice_bitcast_fusion.6), channel_id=1, source_target_pairs={{0,1},{1,2},{2,3},{3,4},{4,5},{5,6},{6,7},{7,8},{8,9},{9,10},{10,1... | collective-permute-start | bytes 122888 | tf_op jit(solution)/shard_map/ppermute | solution.py:36
  33.1 19.3 %collective-permute-start.2 = (f32[64,16,10]{2,1,0:T(8,128)S(1)}, f32[64,16,10]{2,1,0:T(8,128)S(1)}, u32[]{:S(2)}, u32[]{:S(2)}) collective-permute-start(f32[64,16,10]{2,1,0:T(8,128)S(1)} %fusion.112), channel_id=1, source_target_pairs={{0,2},{1,3},{2,4},{3,5},{4,6},{5,7},{6,8},{7,9},{8,10},{9,11},{10,... | collective-permute-start | bytes 122888 | tf_op jit(solution)/shard_map/ppermute | solution.py:36
  52.5 18.3 %collective-permute-start.3 = (f32[64,16,10]{2,1,0:T(8,128)S(1)}, f32[64,16,10]{2,1,0:T(8,128)S(1)}, u32[]{:S(2)}, u32[]{:S(2)}) collective-permute-start(f32[64,16,10]{2,1,0:T(8,128)S(1)} %add.227), channel_id=1, source_target_pairs={{0,4},{1,5},{2,6},{3,7},{4,8},{5,9},{6,10},{7,11},{8,12},{9,13},{1... | collective-permute-start | bytes 122888 | tf_op jit(solution)/shard_map/ppermute | solution.py:36
  70.9 13.7 %collective-permute-start.4 = (f32[64,16,10]{2,1,0:T(8,128)S(1)}, f32[64,16,10]{2,1,0:T(8,128)S(1)}, u32[]{:S(2)}, u32[]{:S(2)}) collective-permute-start(f32[64,16,10]{2,1,0:T(8,128)S(1)} %add.228), channel_id=1, source_target_pairs={{0,8},{1,9},{2,10},{3,11},{4,12},{5,13},{6,14},{7,15},{8,16},{9,17... | collective-permute-start | bytes 122888 | tf_op jit(solution)/shard_map/ppermute | solution.py:36
  84.7 14.6 %collective-permute-start.5 = (f32[64,16,10]{2,1,0:T(8,128)S(1)}, f32[64,16,10]{2,1,0:T(8,128)S(1)}, u32[]{:S(2)}, u32[]{:S(2)}) collective-permute-start(f32[64,16,10]{2,1,0:T(8,128)S(1)} %add.229), channel_id=1, source_target_pairs={{0,16},{1,17},{2,18},{3,19},{4,20},{5,21},{6,22},{7,23},{8,24},{9,... | collective-permute-start | bytes 122888 | tf_op jit(solution)/shard_map/ppermute | solution.py:36
  99.3 26.3 %collective-permute-start.6 = (f32[64,16,10]{2,1,0:T(8,128)S(1)}, f32[64,16,10]{2,1,0:T(8,128)S(1)}, u32[]{:S(2)}, u32[]{:S(2)}) collective-permute-start(f32[64,16,10]{2,1,0:T(8,128)S(1)} %add.230), channel_id=1, source_target_pairs={{0,32},{1,33},{2,34},{3,35},{4,36},{5,37},{6,38},{7,39},{8,40},{9,... | collective-permute-start | bytes 122888 | tf_op jit(solution)/shard_map/ppermute | solution.py:36
  125.7 15.6 %collective-permute-start.7 = (f32[64,16,10]{2,1,0:T(8,128)S(1)}, f32[64,16,10]{2,1,0:T(8,128)S(1)}, u32[]{:S(2)}, u32[]{:S(2)}) collective-permute-start(f32[64,16,10]{2,1,0:T(8,128)S(1)} %add.231), channel_id=1, source_target_pairs={{0,64},{1,65},{2,66},{3,67},{4,68},{5,69},{6,70},{7,71},{8,72},{9,... | collective-permute-start | bytes 122888 | tf_op jit(solution)/shard_map/ppermute | solution.py:36
  134.0 8.4 %copy-start.4 = (f32[64,16,10]{2,1,0:T(8,128)}, f32[64,16,10]{2,1,0:T(8,128)S(1)}, u32[]{:S(2)}) copy-start(f32[64,16,10]{2,1,0:T(8,128)S(1)} %copy.25) | copy-start | bytes 122884
  134.1 8.4 %copy-start.10 = (bf16[256,10]{0,1:T(8,128)(2,1)S(1)}, bf16[256,10]{0,1:T(8,128)(2,1)}, u32[]{:S(2)}) copy-start(bf16[256,10]{0,1:T(8,128)(2,1)} %param.8) | copy-start | bytes 15364
  154.5 5.2 slice-start.4
  155.8 4.0 collective-permute-start.8
  166.0 108.0 %copy-start.1 = (f32[16,64,16,10]{3,2,1,0:T(8,128)S(1)}, f32[16,64,16,10]{3,2,1,0:T(8,128)}, u32[]{:S(2)}) copy-start(f32[16,64,16,10]{3,2,1,0:T(8,128)} %fusion.40) | copy-start | bytes 1966084
  167.2 3.9 collective-permute-start.9
  172.2 17.5 %collective-permute-start.10 = (f32[64,16,10]{2,1,0:T(8,128)S(1)}, f32[64,16,10]{2,1,0:T(8,128)S(1)}, u32[]{:S(2)}, u32[]{:S(2)}) collective-permute-start(f32[64,16,10]{2,1,0:T(8,128)S(1)} %fusion.113), channel_id=1, source_target_pairs={{0,2},{1,3},{2,4},{3,5},{4,6},{5,7},{6,8},{7,9},{8,10},{9,11},{10,... | collective-permute-start | bytes 122888 | tf_op jit(solution)/shard_map/ppermute | solution.py:36
  189.7 17.6 %collective-permute-start.11 = (f32[64,16,10]{2,1,0:T(8,128)S(1)}, f32[64,16,10]{2,1,0:T(8,128)S(1)}, u32[]{:S(2)}, u32[]{:S(2)}) collective-permute-start(f32[64,16,10]{2,1,0:T(8,128)S(1)} %add.241), channel_id=1, source_target_pairs={{0,4},{1,5},{2,6},{3,7},{4,8},{5,9},{6,10},{7,11},{8,12},{9,13},{1... | collective-permute-start | bytes 122888 | tf_op jit(solution)/shard_map/ppermute | solution.py:36
  207.4 14.9 %collective-permute-start.12 = (f32[64,16,10]{2,1,0:T(8,128)S(1)}, f32[64,16,10]{2,1,0:T(8,128)S(1)}, u32[]{:S(2)}, u32[]{:S(2)}) collective-permute-start(f32[64,16,10]{2,1,0:T(8,128)S(1)} %add.242), channel_id=1, source_target_pairs={{0,8},{1,9},{2,10},{3,11},{4,12},{5,13},{6,14},{7,15},{8,16},{9,17... | collective-permute-start | bytes 122888 | tf_op jit(solution)/shard_map/ppermute | solution.py:36
  222.4 9.5 %collective-permute-start.13 = (f32[64,16,10]{2,1,0:T(8,128)S(1)}, f32[64,16,10]{2,1,0:T(8,128)S(1)}, u32[]{:S(2)}, u32[]{:S(2)}) collective-permute-start(f32[64,16,10]{2,1,0:T(8,128)S(1)} %add.243), channel_id=1, source_target_pairs={{0,16},{1,17},{2,18},{3,19},{4,20},{5,21},{6,22},{7,23},{8,24},{9,... | collective-permute-start | bytes 122888 | tf_op jit(solution)/shard_map/ppermute | solution.py:36
  232.0 25.6 %collective-permute-start.14 = (f32[64,16,10]{2,1,0:T(8,128)S(1)}, f32[64,16,10]{2,1,0:T(8,128)S(1)}, u32[]{:S(2)}, u32[]{:S(2)}) collective-permute-start(f32[64,16,10]{2,1,0:T(8,128)S(1)} %add.244), channel_id=1, source_target_pairs={{0,32},{1,33},{2,34},{3,35},{4,36},{5,37},{6,38},{7,39},{8,40},{9,... | collective-permute-start | bytes 122888 | tf_op jit(solution)/shard_map/ppermute | solution.py:36
  257.7 23.0 %copy-start.5 = (f32[64,16,10]{2,1,0:T(8,128)S(1)}, f32[64,16,10]{2,1,0:T(8,128)}, u32[]{:S(2)}) copy-start(f32[64,16,10]{2,1,0:T(8,128)} %copy-done.4) | copy-start | bytes 122884
  257.7 22.9 %collective-permute-start.15 = (f32[64,16,10]{2,1,0:T(8,128)S(1)}, f32[64,16,10]{2,1,0:T(8,128)S(1)}, u32[]{:S(2)}, u32[]{:S(2)}) collective-permute-start(f32[64,16,10]{2,1,0:T(8,128)S(1)} %add.245), channel_id=1, source_target_pairs={{0,64},{1,65},{2,66},{3,67},{4,68},{5,69},{6,70},{7,71},{8,72},{9,... | collective-permute-start | bytes 122888 | tf_op jit(solution)/shard_map/ppermute | solution.py:36
  292.7 5.2 slice-start.5
  294.0 4.0 collective-permute-start.16
  304.1 109.1 %copy-start.2 = (f32[16,64,16,10]{3,2,1,0:T(8,128)S(1)}, f32[16,64,16,10]{3,2,1,0:T(8,128)}, u32[]{:S(2)}) copy-start(f32[16,64,16,10]{3,2,1,0:T(8,128)} %fusion.45) | copy-start | bytes 1966084
  305.4 4.6 collective-permute-start.17
  311.1 17.5 %collective-permute-start.18 = (f32[64,16,10]{2,1,0:T(8,128)S(1)}, f32[64,16,10]{2,1,0:T(8,128)S(1)}, u32[]{:S(2)}, u32[]{:S(2)}) collective-permute-start(f32[64,16,10]{2,1,0:T(8,128)S(1)} %fusion.114), channel_id=1, source_target_pairs={{0,2},{1,3},{2,4},{3,5},{4,6},{5,7},{6,8},{7,9},{8,10},{9,11},{10,... | collective-permute-start | bytes 122888 | tf_op jit(solution)/shard_map/ppermute | solution.py:36
  328.6 14.7 %collective-permute-start.19 = (f32[64,16,10]{2,1,0:T(8,128)S(1)}, f32[64,16,10]{2,1,0:T(8,128)S(1)}, u32[]{:S(2)}, u32[]{:S(2)}) collective-permute-start(f32[64,16,10]{2,1,0:T(8,128)S(1)} %add.255), channel_id=1, source_target_pairs={{0,4},{1,5},{2,6},{3,7},{4,8},{5,9},{6,10},{7,11},{8,12},{9,13},{1... | collective-permute-start | bytes 122888 | tf_op jit(solution)/shard_map/ppermute | solution.py:36
  343.4 13.3 %collective-permute-start.20 = (f32[64,16,10]{2,1,0:T(8,128)S(1)}, f32[64,16,10]{2,1,0:T(8,128)S(1)}, u32[]{:S(2)}, u32[]{:S(2)}) collective-permute-start(f32[64,16,10]{2,1,0:T(8,128)S(1)} %add.256), channel_id=1, source_target_pairs={{0,8},{1,9},{2,10},{3,11},{4,12},{5,13},{6,14},{7,15},{8,16},{9,17... | collective-permute-start | bytes 122888 | tf_op jit(solution)/shard_map/ppermute | solution.py:36
  356.8 15.6 %collective-permute-start.21 = (f32[64,16,10]{2,1,0:T(8,128)S(1)}, f32[64,16,10]{2,1,0:T(8,128)S(1)}, u32[]{:S(2)}, u32[]{:S(2)}) collective-permute-start(f32[64,16,10]{2,1,0:T(8,128)S(1)} %add.257), channel_id=1, source_target_pairs={{0,16},{1,17},{2,18},{3,19},{4,20},{5,21},{6,22},{7,23},{8,24},{9,... | collective-permute-start | bytes 122888 | tf_op jit(solution)/shard_map/ppermute | solution.py:36
  372.4 23.4 %collective-permute-start.22 = (f32[64,16,10]{2,1,0:T(8,128)S(1)}, f32[64,16,10]{2,1,0:T(8,128)S(1)}, u32[]{:S(2)}, u32[]{:S(2)}) collective-permute-start(f32[64,16,10]{2,1,0:T(8,128)S(1)} %add.258), channel_id=1, source_target_pairs={{0,32},{1,33},{2,34},{3,35},{4,36},{5,37},{6,38},{7,39},{8,40},{9,... | collective-permute-start | bytes 122888 | tf_op jit(solution)/shard_map/ppermute | solution.py:36
  395.9 24.1 %copy-start.6 = (f32[64,16,10]{2,1,0:T(8,128)S(1)}, f32[64,16,10]{2,1,0:T(8,128)}, u32[]{:S(2)}) copy-start(f32[64,16,10]{2,1,0:T(8,128)} %copy-done.4) | copy-start | bytes 122884
  395.9 24.0 %collective-permute-start.23 = (f32[64,16,10]{2,1,0:T(8,128)S(1)}, f32[64,16,10]{2,1,0:T(8,128)S(1)}, u32[]{:S(2)}, u32[]{:S(2)}) collective-permute-start(f32[64,16,10]{2,1,0:T(8,128)S(1)} %add.259), channel_id=1, source_target_pairs={{0,64},{1,65},{2,66},{3,67},{4,68},{5,69},{6,70},{7,71},{8,72},{9,... | collective-permute-start | bytes 122888 | tf_op jit(solution)/shard_map/ppermute | solution.py:36
  432.0 5.2 slice-start.3
  433.3 4.0 collective-permute-start.24
  444.5 4.4 collective-permute-start.25
  450.0 17.5 %collective-permute-start.26 = (f32[64,16,10]{2,1,0:T(8,128)S(1)}, f32[64,16,10]{2,1,0:T(8,128)S(1)}, u32[]{:S(2)}, u32[]{:S(2)}) collective-permute-start(f32[64,16,10]{2,1,0:T(8,128)S(1)} %fusion.115), channel_id=1, source_target_pairs={{0,2},{1,3},{2,4},{3,5},{4,6},{5,7},{6,8},{7,9},{8,10},{9,11},{10,... | collective-permute-start | bytes 122888 | tf_op jit(solution)/shard_map/ppermute | solution.py:36
  467.5 14.7 %collective-permute-start.27 = (f32[64,16,10]{2,1,0:T(8,128)S(1)}, f32[64,16,10]{2,1,0:T(8,128)S(1)}, u32[]{:S(2)}, u32[]{:S(2)}) collective-permute-start(f32[64,16,10]{2,1,0:T(8,128)S(1)} %add.269), channel_id=1, source_target_pairs={{0,4},{1,5},{2,6},{3,7},{4,8},{5,9},{6,10},{7,11},{8,12},{9,13},{1... | collective-permute-start | bytes 122888 | tf_op jit(solution)/shard_map/ppermute | solution.py:36
  482.3 13.3 %collective-permute-start.28 = (f32[64,16,10]{2,1,0:T(8,128)S(1)}, f32[64,16,10]{2,1,0:T(8,128)S(1)}, u32[]{:S(2)}, u32[]{:S(2)}) collective-permute-start(f32[64,16,10]{2,1,0:T(8,128)S(1)} %add.270), channel_id=1, source_target_pairs={{0,8},{1,9},{2,10},{3,11},{4,12},{5,13},{6,14},{7,15},{8,16},{9,17... | collective-permute-start | bytes 122888 | tf_op jit(solution)/shard_map/ppermute | solution.py:36
  495.6 17.5 %collective-permute-start.29 = (f32[64,16,10]{2,1,0:T(8,128)S(1)}, f32[64,16,10]{2,1,0:T(8,128)S(1)}, u32[]{:S(2)}, u32[]{:S(2)}) collective-permute-start(f32[64,16,10]{2,1,0:T(8,128)S(1)} %add.271), channel_id=1, source_target_pairs={{0,16},{1,17},{2,18},{3,19},{4,20},{5,21},{6,22},{7,23},{8,24},{9,... | collective-permute-start | bytes 122888 | tf_op jit(solution)/shard_map/ppermute | solution.py:36
  513.2 46.0 %slice-start = ((s8[8388608]{0:T(1024)(128)(4,1)}), s8[4194304]{0:T(1024)(128)(4,1)S(1)}, s32[]{:S(2)}) async-start(s8[8388608]{0:T(1024)(128)(4,1)} %bitcast.63), calls=%async_computation | async-start | bytes 8388608
  513.2 21.8 %collective-permute-start.30 = (f32[64,16,10]{2,1,0:T(8,128)S(1)}, f32[64,16,10]{2,1,0:T(8,128)S(1)}, u32[]{:S(2)}, u32[]{:S(2)}) collective-permute-start(f32[64,16,10]{2,1,0:T(8,128)S(1)} %add.272), channel_id=1, source_target_pairs={{0,32},{1,33},{2,34},{3,35},{4,36},{5,37},{6,38},{7,39},{8,40},{9,... | collective-permute-start | bytes 122888 | tf_op jit(solution)/shard_map/ppermute | solution.py:36
  535.1 24.2 %slice-start.1 = ((s8[8388608]{0:T(1024)(128)(4,1)}), s8[4194304]{0:T(1024)(128)(4,1)S(1)}, s32[]{:S(2)}) async-start(s8[8388608]{0:T(1024)(128)(4,1)} %bitcast.63), calls=%async_computation.1 | async-start | bytes 8388608
  535.1 24.3 %slice-start.2 = ((f32[16,64,16,10]{3,2,1,0:T(8,128)}), f32[15,64,16,10]{3,2,1,0:T(8,128)S(1)}, s32[]{:S(2)}) async-start(f32[16,64,16,10]{3,2,1,0:T(8,128)} %fusion.50), calls=%async_computation.2 | async-start | bytes 15728640 | tf_op jit(solution)/shard_map/slice | solution.py:32
  535.1 24.3 %copy-start.7 = (f32[64,16,10]{2,1,0:T(8,128)S(1)}, f32[64,16,10]{2,1,0:T(8,128)}, u32[]{:S(2)}) copy-start(f32[64,16,10]{2,1,0:T(8,128)} %copy-done.4) | copy-start | bytes 122884
  535.1 24.1 %collective-permute-start.31 = (f32[64,16,10]{2,1,0:T(8,128)S(1)}, f32[64,16,10]{2,1,0:T(8,128)S(1)}, u32[]{:S(2)}, u32[]{:S(2)}) collective-permute-start(f32[64,16,10]{2,1,0:T(8,128)S(1)} %add.273), channel_id=1, source_target_pairs={{0,64},{1,65},{2,66},{3,67},{4,68},{5,69},{6,70},{7,71},{8,72},{9,... | collective-permute-start | bytes 122888 | tf_op jit(solution)/shard_map/ppermute | solution.py:36
  (2 other events, 3.4 us)
where the time goes:
time: 572 us; the launch traced here: 570 us
  starting transfers between devices  244 us (43%)
  waiting for transfers between devices  209 us (37%)
  matrix products  43.4 us (8%)
  other arithmetic  38.6 us (7%)
  local copies, waits for them, and re-layouts  33.8 us (6%)
    ppermute x28, starting transfers between devices, local(): lax.ppermute(inclusive, 'time', [(source, source + distance) for source i...  238 us
    ppermute x28, waiting for transfers between devices, local(): lax.ppermute(inclusive, 'time', [(source, source + distance) for source i...  202 us
    dot_general x4, matrix products, drift_block(): jnp.einsum('kbnd,dc->kbnc', hidden_act.astype(jnp.bfloat16), w_out, prefe...  43.1 us
    another operation x4, other arithmetic, local(): local_cum = jnp.cumsum(increments, axis=0)  24.7 us
    slice x5, local copies, waits for them, and re-layouts, local(): local_cum[:-1]  15 us
  transfers between devices with their start and end apart: 32, of which 31 were waited for; matrix products, arithmetic and copies ran while one was open for 3% of the time, Pallas kernels for 0%

commit v1 on v0

v1 whole, which is shorter than its diff:
```python
import functools

import jax
import jax.numpy as jnp
from jax import lax
from jax.experimental import pallas as pl
from jax.experimental.pallas import tpu as pltpu
from jax.sharding import PartitionSpec as P

CUBE = 0.044715
ROOT = 0.7978845608028654
F32, BF16 = jnp.float32, jnp.bfloat16

def nn(a, b):
    return lax.dot_general(a, b, (((1,), (0,)), ((), ())), preferred_element_type=F32)

def act(y):
    q = y * ((2.0 * ROOT) + (8.0 * ROOT * CUBE) * (y * y))
    return (y + y * jnp.tanh(q)).astype(BF16)

def body(ms, mt, hs, x0, xr, wi, wo, tri, out, sf, bf, xrow, db, *accs, scan_u=8):
    ys, ds, es = accs[:4], accs[4:8], accs[8:]
    db[128] = jnp.zeros((16, 128), F32)
    xrow[...] = jnp.zeros_like(xrow)
    x0v = x0[...]
    wov = wo[...]

    def conv(i, _):
        r = pl.ds(pl.multiple_of(i * 64, 64), 64)
        sf[r, :] = 0.5 + 0.5 * ms[r, :].astype(F32)
        bf[r, :] = 0.5 * mt[r, :].astype(F32)
        return 0
    lax.fori_loop(0, 32, conv, 0)

    def rowpair(ref, r):
        a = jnp.broadcast_to(ref[pl.ds(r, 1), :], (8, 256))
        b = jnp.broadcast_to(ref[pl.ds(r + 1, 1), :], (8, 256))
        return jnp.concatenate([a, b], axis=0)

    def hidden(t, y_of):
        hs_ = []
        for k in range(16):
            r = t * 32 + 2 * k
            hs_.append(act(y_of(k) * rowpair(sf, r) + rowpair(bf, r)))
        return jnp.concatenate(hs_, axis=0)

    def put(t, d):
        db[2 * t] = d[:, :128]
        db[2 * t + 1] = d[:, 128:]

    def xt(t):
        v = xrow[pl.ds(pl.multiple_of(t * 256, 256), 256), :]
        return jnp.concatenate([v, jnp.zeros((256, 128), BF16)], axis=1)

    for r in accs:
        pltpu.matmul_pop(r)
    pltpu.matmul_push_rhs(wi[...], staging_register=0, mxu_index=0)
    pltpu.matmul_acc_lhs(ys[0], xr[...], load_staged_rhs=0)
    u = pltpu.matmul_pop(ys[0])[:8]

    def sweep(first):
        if not first:
            pltpu.matmul_push_rhs(wi[...], staging_register=0, mxu_index=0)
            pltpu.matmul_acc_lhs(ys[0], xt(0), load_staged_rhs=0)
            pltpu.matmul_acc_lhs(ys[1], xt(1))
        def step(i, _):
            for s in range(4):
                t = 4 * i + s
                if first:
                    uu = jnp.concatenate([u, u], axis=0)
                    h = hidden(t, lambda k: uu)
                else:
                    pltpu.matmul_acc_lhs(ys[(s + 2) % 4], xt(jnp.minimum(t + 2, 63)))
                    y = pltpu.matmul_pop(ys[s])
                    h = hidden(t, lambda k: y[16 * k:16 * k + 16])
                pltpu.matmul_push_rhs(h, staging_register=s % 2, mxu_index=1, transpose=True)
                pltpu.matmul_acc_lhs(ds[s], wov, load_staged_rhs=s % 2)
                put(lax.rem(t + 62, 64), pltpu.matmul_pop(ds[(s + 2) % 4]))
            return 0
        lax.fori_loop(0, 16, step, 0)
        put(62, pltpu.matmul_pop(ds[2]))
        put(63, pltpu.matmul_pop(ds[3]))
        if not first:
            pltpu.matmul_pop(ys[0])
            pltpu.matmul_pop(ys[1])

    lane = lax.broadcasted_iota(jnp.int32, (16, 128), 1)
    zb = jnp.zeros((16, 128), BF16)
    def scan(last):
        pltpu.matmul_push_rhs(tri[...], staging_register=0, mxu_index=1)
        def feed(k, e, load=None):
            for i in range(8):
                t = k * 8 + i
                d = db[t]
                dn = jnp.where(lane < 120, pltpu.roll(d, 120, 1), pltpu.roll(db[t + 1], 120, 1))
                g = (d + dn) * hs[pl.ds(t, 1), :]
                hi = g.astype(BF16)
                r1 = g - hi.astype(F32)
                mid = r1.astype(BF16)
                lo = (r1 - mid.astype(F32)).astype(BF16)
                pltpu.matmul_acc_lhs(e[i], jnp.concatenate([hi, mid], axis=1), load_staged_rhs=load if i == 0 else None)
                pltpu.matmul_acc_lhs(e[i], jnp.concatenate([lo, zb], axis=1))
        def drain(k, e, carry):
            for i in range(8):
                t = k * 8 + i
                pr = pltpu.matmul_pop(e[i])
                x = carry + pr[:, :128]
                carry = carry + pr[:, 128:]
                if last:
                    out[t] = x
                else:
                    xrow[pl.ds(pl.multiple_of(t * 128, 128), 128), 0:16] = x.T.astype(BF16)
            return carry
        feed(0, es[:8], 0)
        def step(k, carry):
            feed(2 * k + 1, es[8:])
            carry = drain(2 * k, es[:8], carry)
            feed(jnp.minimum(2 * k + 2, 15), es[:8])
            return drain(2 * k + 1, es[8:], carry)
        lax.fori_loop(0, 8, step, x0v)
        for e in es[:8]:
            pltpu.matmul_pop(e)

    sweep(True)
    for _ in range(3):
        scan(False)
        sweep(False)
    scan(True)

def kernel(*refs, **kw):
    pl.run_scoped(functools.partial(body, *refs, **kw),
                  *[pltpu.ACC(0)((256, 256), F32)] * 4, *[pltpu.ACC(1)((16, 256), F32)] * 20)

def call(ms, mt, hs, x0, xr, wi, wo, tri, **kw):
    v = pl.BlockSpec(memory_space=pltpu.VMEM)
    return pl.pallas_call(
        functools.partial(kernel, **kw),
        out_shape=jax.ShapeDtypeStruct((128, 16, 128), F32),
        in_specs=[v] * 8, out_specs=v,
        scratch_shapes=[
            pltpu.VMEM((2048, 256), F32), pltpu.VMEM((2048, 256), F32),
            pltpu.VMEM((16384, 128), BF16), pltpu.VMEM((129, 16, 128), F32)],
        compiler_params=pltpu.CompilerParams(vmem_limit_bytes=60 * 2**20),
    )(ms, mt, hs, x0, xr, wi, wo, tri)


def triangle():
    i = jnp.arange(128)
    same = (i[:, None] % 8) == (i[None, :] % 8)
    strict = same & ((i[:, None] // 8) < (i[None, :] // 8))
    t = 256.0 * jnp.concatenate([strict, same], axis=1).astype(F32)
    return jnp.concatenate([t, t], axis=0).astype(BF16)

def untangle(src, out):
    for c in range(10):
        for half in range(2):
            m = src[half, :, c, :].T
            for k in range(16):
                out[k, c, 8 * half:8 * half + 8, :] = m[8 * k:8 * k + 8, :]

def solution(mesh):
    def local(x_init, w_in, w_out, mod_scale, mod_shift, step_size):
        me = lax.axis_index("time")
        half, batch = me // 64, me % 64
        xr = lax.dynamic_slice(x_init, (batch, half * 8, 0), (1, 8, 10))[0]
        ms = lax.all_gather(mod_scale, "time", axis=0, tiled=True)
        mt = lax.all_gather(mod_shift, "time", axis=0, tiled=True)
        st = lax.all_gather(step_size, "time", axis=0, tiled=True)
        x0 = jnp.pad(jnp.tile(xr.T, (1, 16)), ((0, 6), (0, 0)))
        xp = jnp.pad(xr, ((0, 248), (0, 246))).astype(BF16)
        wi = jnp.pad(w_in, ((0, 246), (0, 0)))
        wo = jnp.pad(w_out.T, ((0, 6), (0, 0)))
        hs = jnp.repeat(st * (0.5 / 256.0), 8).reshape(128, 128)
        mine = call(ms, mt, hs, x0, xp, wi, wo, triangle())
        got = lax.all_to_all(mine, "time", 0, 0, tiled=True)
        v = pl.BlockSpec(memory_space=pltpu.VMEM)
        res = pl.pallas_call(untangle, out_shape=jax.ShapeDtypeStruct((16, 10, 16, 64), F32), in_specs=[v], out_specs=v)(got.reshape(2, 64, 16, 128))
        return jnp.transpose(res, (0, 3, 2, 1))

    return jax.shard_map(local, mesh=mesh, in_specs=(P("data"), P(), P(), P("time"), P("time"), P("time")), out_specs=P("time", "data"), check_vma=False)
```

time: 572 us -> 215 us (0.38)
  the two profiles are of different devices: /device:TPU:0 before, /device:TPU:1 now
where the time goes in v1:
time: 215 us
  blocking collectives  94 us (44%)
  waiting for transfers between devices  58.2 us (27%)
  Pallas kernels  42 us (20%)
  between operations  13.5 us (6%)
  local copies, waits for them, and re-layouts  6.15 us (3%)
    unnamed x1, blocking collectives  69.5 us
    all_gather x1, waiting for transfers between devices, local(): mt = lax.all_gather(mod_shift, 'time', axis=0, tiled=True)  56.8 us
    pallas_call x1, Pallas kernels, call(): pl.pallas_call(functools.partial(kernel, **kw), out_shape=jax.ShapeDtypeS...  39.3 us
    all_to_all x1, blocking collectives, local(): got = lax.all_to_all(mine, 'time', 0, 0, tiled=True)  24.5 us
  transfers between devices with their start and end apart: 2, of which 1 were waited for; matrix products, arithmetic and copies ran while one was open for 3% of the time, Pallas kernels for 0%

profile of v1, /device:TPU:1, one launch (start us, length us, event | category | flops | bytes accessed | tf_op | source)
XLA Modules:
  0.0 214.7 jit_solution(10310907003258630856)
XLA Ops:
  6.5 0.0 copy-start
  6.5 0.0 all-gather.3.cloned.1.call-start
  6.5 0.7 all-gather.3.cloned.1.call-update
  7.3 0.0 all-gather.5.cloned.1.call-start
  7.3 0.7 all-gather.5.cloned.1.call-update
  8.0 0.0 copy-done
  8.1 0.1 constant_dynamic-slice_fusion
  8.1 0.1 copy.13
  8.3 0.2 copy.14
  8.4 0.9 dynamic-update-slice
  9.3 69.5 %all-reduce.4 = f32[2048]{0:T(1024)S(1)} all-reduce(f32[2048]{0:T(1024)S(1)} %dynamic-update-slice), channel_id=1, replica_groups=mesh['data'=1,'time'=128] {'time'}, use_global_device_ids=true, to_apply=%add.4 | all-reduce | flops 2048 | bytes 16384
  78.8 0.1 broadcast_in_dim.11
  78.9 0.1 copy.9
  79.0 0.7 copy.12.refs_2_
  79.7 0.1 tile.10
  79.8 0.6 pad.17.refs_3_
  80.4 1.3 pad.20.refs_6_
  81.7 0.7 pad.18.refs_4_
  82.4 1.4 pad.19.refs_5_
  83.7 0.1 compare_and_fusion
  83.9 0.7 pad_maximum_fusion.refs_7_
  84.5 0.0 all-gather.3.cloned.1.call-done.refs_0_
  84.5 56.8 %all-gather.5.cloned.1.call-done.refs_1_ = bf16[2048,256]{1,0:T(8,128)(2,1)} async-done(((bf16[16,256]{1,0:T(8,128)(2,1)}), bf16[2048,256]{1,0:T(8,128)(2,1)}) %all-gather.5.cloned.1.call-update) | async-done | bytes 1048592 | tf_op jit(solution)/shard_map/all_gather | solution.py:167
  141.3 39.3 %shard_map.64 = f32[128,16,128]{2,1,0:T(8,128)} custom-call(bf16[2048,256]{1,0:T(8,128)(2,1)} %all-gather.3.cloned.1.call-done.refs_0_, bf16[2048,256]{1,0:T(8,128)(2,1)} %all-gather.5.cloned.1.call-done.refs_1_, f32[128,128]{1,0:T(8,128)} %copy.12.refs_2_, f32[16,128]{1,0:T(8,128)} %pad.17.refs_3_, bf16[256,256]{1,0:T(8,128)(2,1)} %pad.18.refs_4_, ...), custom_call_target="tpu_custom_call" | custom-call | tf_op jit(solution)/shard_map/pallas_call | solution.py:136
  180.6 24.5 %all_to_all.5 = f32[128,16,128]{2,1,0:T(8,128)} all-to-all(f32[128,16,128]{2,1,0:T(8,128)} %shard_map.64), channel_id=1, replica_groups=mesh['data'=1,'time'=128] {'time'}, dimensions={0} | all-to-all | bytes 2097152 | tf_op jit(solution)/shard_map/all_to_all | solution.py:175
  205.1 2.7 %shard_map.65 = f32[16,10,16,64]{3,2,1,0:T(8,128)} custom-call(f32[2,64,16,128]{3,2,1,0:T(8,128)} %bitcast.11), custom_call_target="tpu_custom_call" | custom-call | tf_op jit(solution)/shard_map/pallas_call | solution.py:177
  (6 shorter events, 0.0 us)
Async XLA Ops:
  6.5 1.5 copy-start
  6.5 78.0 %all-gather.3.cloned.1.call-start = ((), (), s32[]{:S(2)}) async-start(), calls=%async_computation.1 | async-start | bytes 1056768 | tf_op jit(solution)/shard_map/all_gather | solution.py:166
  7.3 134.0 %all-gather.5.cloned.1.call-start = ((), (), s32[]{:S(2)}) async-start(), calls=%async_computation.2 | async-start | bytes 1056768 | tf_op jit(solution)/shard_map/all_gather | solution.py:167
Sparse Core Ops, SparseCore 0:
  10.1 67.2 all-gather.2
  80.2 61.0 all-gather.4

commit v2 on v1

--- a/solution.py
+++ b/solution.py
@@ -7,6 +7,7 @@
 from jax.experimental.pallas import tpu as pltpu
 from jax.sharding import PartitionSpec as P
 
+MESH = pl.DeviceIdType.MESH
 CUBE = 0.044715
 ROOT = 0.7978845608028654
 F32, BF16 = jnp.float32, jnp.bfloat16
@@ -18,19 +19,47 @@
     q = y * ((2.0 * ROOT) + (8.0 * ROOT * CUBE) * (y * y))
     return (y + y * jnp.tanh(q)).astype(BF16)
 
-def body(ms, mt, hs, x0, xr, wi, wo, tri, out, sf, bf, xrow, db, *accs, scan_u=8):
-    ys, ds, es = accs[:4], accs[4:8], accs[8:]
+def body(buf, hs, xt_, w_in, w_out, out, sf, bf, xrow, db, wi, wo, tris, *accs):
+    ys, ds, es = accs[:4], accs[4:8], accs[8:24]
+    u_acc = accs[24]
     db[128] = jnp.zeros((16, 128), F32)
     xrow[...] = jnp.zeros_like(xrow)
-    x0v = x0[...]
+    me = lax.axis_index("time")
+    core = me % 2
+    half, batch = me // 64, me % 64
+    wi[...] = jnp.zeros_like(wi)
+    wo[...] = jnp.zeros_like(wo)
+    wi[0:10, :] = w_in[...]
+    wo[0:10, :] = w_out[...]
+    lane8 = lax.broadcasted_iota(jnp.int32, (8, 128), 1)
+    pick = lax.broadcasted_iota(jnp.int32, (8, 64), 1) == batch
+    xr = jnp.zeros((8, 128), F32)
+    for ch in range(10):
+        col = jnp.sum(jnp.where(pick, xt_[ch, pl.ds(pl.multiple_of(half * 8, 8), 8), :], 0.0), axis=1, keepdims=True)
+        xr = jnp.where(lane8 == ch, col, xr)
+    x0v = jnp.concatenate([xr] * 16, axis=0).T[0:16, :]
+    xl = jnp.concatenate([jnp.concatenate([xr, jnp.zeros((8, 128), F32)], axis=0).astype(BF16), jnp.zeros((16, 128), BF16)], axis=1)
+    ri = lax.broadcasted_iota(jnp.int32, (256, 256), 0) % 128
+    ci = lax.broadcasted_iota(jnp.int32, (256, 256), 1)
+    cm = ci % 128
+    tri = jnp.where(((ri % 8) == (cm % 8)) & ((ci >= 128) | ((ri // 8) < (cm // 8))), 256.0, 0.0).astype(BF16)
+    tris[...] = tri
+    for r in accs:
+        pltpu.matmul_pop(r)
+    pltpu.matmul_push_rhs(wi[...], staging_register=0, mxu_index=1)
+    pltpu.matmul_acc_lhs(u_acc, xl, load_staged_rhs=0)
+    u = pltpu.matmul_pop(u_acc)[:8]
     wov = wo[...]
 
-    def conv(i, _):
-        r = pl.ds(pl.multiple_of(i * 64, 64), 64)
-        sf[r, :] = 0.5 + 0.5 * ms[r, :].astype(F32)
-        bf[r, :] = 0.5 * mt[r, :].astype(F32)
+    def other(t):
+        return (t % 4) * 16 + ((t // 4) % 4) * 4 + t // 16
+
+    def conv(t, _):
+        r = pl.ds(pl.multiple_of(t * 32, 32), 32)
+        sf[r, :] = 0.5 + 0.5 * buf[0, t].astype(F32)
+        bf[r, :] = 0.5 * buf[1, other(t)].astype(F32)
         return 0
-    lax.fori_loop(0, 32, conv, 0)
+    lax.fori_loop(0, 64, conv, 0)
 
     def rowpair(ref, r):
         a = jnp.broadcast_to(ref[pl.ds(r, 1), :], (8, 256))
@@ -51,12 +80,6 @@
     def xt(t):
         v = xrow[pl.ds(pl.multiple_of(t * 256, 256), 256), :]
         return jnp.concatenate([v, jnp.zeros((256, 128), BF16)], axis=1)
-
-    for r in accs:
-        pltpu.matmul_pop(r)
-    pltpu.matmul_push_rhs(wi[...], staging_register=0, mxu_index=0)
-    pltpu.matmul_acc_lhs(ys[0], xr[...], load_staged_rhs=0)
-    u = pltpu.matmul_pop(ys[0])[:8]
 
     def sweep(first):
         if not first:
@@ -87,13 +110,15 @@
     lane = lax.broadcasted_iota(jnp.int32, (16, 128), 1)
     zb = jnp.zeros((16, 128), BF16)
     def scan(last):
-        pltpu.matmul_push_rhs(tri[...], staging_register=0, mxu_index=1)
+        pltpu.matmul_push_rhs(tris[...], staging_register=0, mxu_index=1)
         def feed(k, e, load=None):
             for i in range(8):
                 t = k * 8 + i
+                tile = k * 4 + i // 2
+                tile = tile + core * (other(tile) - tile)
                 d = db[t]
                 dn = jnp.where(lane < 120, pltpu.roll(d, 120, 1), pltpu.roll(db[t + 1], 120, 1))
-                g = (d + dn) * hs[pl.ds(t, 1), :]
+                g = (d + dn) * hs[tile, i % 2]
                 hi = g.astype(BF16)
                 r1 = g - hi.astype(F32)
                 mid = r1.astype(BF16)
@@ -129,27 +154,168 @@
 
 def kernel(*refs, **kw):
     pl.run_scoped(functools.partial(body, *refs, **kw),
-                  *[pltpu.ACC(0)((256, 256), F32)] * 4, *[pltpu.ACC(1)((16, 256), F32)] * 20)
-
-def call(ms, mt, hs, x0, xr, wi, wo, tri, **kw):
+                  *[pltpu.ACC(0)((256, 256), F32)] * 4, *[pltpu.ACC(1)((16, 256), F32)] * 20, pltpu.ACC(1)((16, 256), F32))
+
+
+def gather_kernel(ms, mt, st, buf, hs, own, hrow, sx, rx, sh, rh, sm, rm, sd, rd):
+    me = lax.axis_index("time")
+    core = me % 2
+    x, y, z = (me // 2) % 4, (me // 8) % 4, me // 32
+    a = x + core * (z - x)
+    b = y
+    c = z + core * (x - z)
+    ka, kc = 1 + 15 * core, 16 - 15 * core
+
+    def dev(da, db, dc):
+        aa, bb, cc = (a + da) % 4, (b + db) % 4, (c + dc) % 4
+        return 2 * (aa * ka + bb * 4 + cc * kc) + core
+
+    def idx(da, db, dc):
+        return ((c + dc) % 4) * 16 + ((b + db) % 4) * 4 + (a + da) % 4
+
+    partner = me + 1 - 2 * core
+    peers = [dev(1, 0, 0), dev(3, 0, 0), dev(2, 0, 0), dev(0, 1, 0), dev(0, 3, 0), dev(0, 2, 0),
+             dev(0, 0, 1), dev(0, 0, 3), dev(0, 0, 2), partner]
+    own[0] = ms[...]
+    own[1] = mt[...]
+    lane = lax.broadcasted_iota(jnp.int32, (1, 128), 1)
+    row = jnp.zeros((1, 128), F32)
+    for k in range(16):
+        row = jnp.where(lane // 8 == k, st[k] * (0.5 / 256.0), row)
+    hrow[...] = row
+
+    barrier = pltpu.get_barrier_semaphore()
+    for p in peers:
+        pl.semaphore_signal(barrier, inc=1, device_id={"time": p}, device_id_type=MESH)
+    pl.semaphore_wait(barrier, len(peers))
+
+    def remote(src, dst, s, r, p):
+        cp = pltpu.make_async_remote_copy(src_ref=src, dst_ref=dst, send_sem=s, recv_sem=r,
+                                          device_id={"time": p}, device_id_type=MESH)
+        cp.start()
+        return cp
+
+    mine = idx(0, 0, 0)
+    sent = []
+    half = pl.ds(pl.multiple_of(core * 16, 16), 16)
+    other = pl.ds(pl.multiple_of(16 - core * 16, 16), 16)
+    ex = remote(own.at[1 - core], buf.at[1 - core, idx_of(me, 1 - core), half], sx.at[0], rx.at[0], partner)
+    hx = remote(hrow, hs.at[idx_of(me, 1 - core), core], sx.at[1], rx.at[1], partner)
+    l1 = pltpu.make_async_copy(own.at[core], buf.at[core, mine, half], sx.at[2])
+    l2 = pltpu.make_async_copy(hrow, hs.at[mine, core], sx.at[3])
+    l1.start(); l2.start()
+    ex.wait(); hx.wait(); l1.wait(); l2.wait()
+
+    nsend = [0]
+    def send(i, p):
+        k = nsend[0]
+        nsend[0] += 1
+        sent.append(remote(buf.at[core, i], buf.at[core, i], sm.at[k], rm.at[i], p))
+    def relay(i, k):
+        sent.append(remote(buf.at[core, i], buf.at[core, i], sd.at[k], rd.at[i], partner))
+    def arrive(i):
+        pltpu.make_async_copy(buf.at[core, i], buf.at[core, i], rm.at[i]).wait()
+
+    hn = [0]
+    def hsend(ref, j, p):
+        k = hn[0]
+        hn[0] += 1
+        sent.append(remote(ref, ref, sh.at[k], rh.at[k], p))
+    def harrive(ref, k):
+        pltpu.make_async_copy(ref, ref, rh.at[k]).wait()
+
+    order = (0, 1, 3, 2)
+    for d in order[1:]:
+        send(mine, dev(d, 0, 0))
+    hm = hs.at[mine]
+    for d in order[1:]:
+        hsend(hm, d, dev(d, 0, 0))
+    relay(mine, 0)
+    nrel = 1
+    for da in order:
+        i = idx(da, 0, 0)
+        if da:
+            arrive(i)
+        for d in order[1:]:
+            send(i, dev(0, d, 0))
+        for d in (1, 3):
+            send(i, dev(0, 0, d))
+        if da:
+            relay(i, nrel)
+            nrel += 1
+    for k, d in enumerate(order[1:]):
+        harrive(hs.at[idx(-d % 4, 0, 0)], k)
+    hb = hs.at[pl.ds(pl.multiple_of(c * 16 + b * 4, 4), 4)]
+    for d in order[1:]:
+        hsend(hb, d, dev(0, d, 0))
+    for db in order[1:]:
+        for da in order:
+            i = idx(da, db, 0)
+            arrive(i)
+            for d in (1, 3):
+                send(i, dev(0, 0, d))
+            relay(i, nrel)
+            nrel += 1
+    for k, d in enumerate(order[1:]):
+        harrive(hs.at[pl.ds(pl.multiple_of(c * 16 + ((b - d) % 4) * 4, 4), 4)], 3 + k)
+    hc = hs.at[pl.ds(pl.multiple_of(c * 16, 16), 16)]
+    for d in order[1:]:
+        hsend(hc, d, dev(0, 0, d))
+    n = 0
+    for db in order:
+        for da in order:
+            for dc, step in ((3, 1), (1, 3)):
+                i = idx(da, db, dc)
+                arrive(i)
+                if (n < 8) == (step == 1):
+                    send(i, dev(0, 0, step))
+                relay(i, nrel)
+                nrel += 1
+            n += 1
+    for db in order:
+        for da in order:
+            i = idx(da, db, 2)
+            arrive(i)
+            relay(i, nrel)
+            nrel += 1
+    for k, d in enumerate(order[1:]):
+        harrive(hs.at[pl.ds(pl.multiple_of(((c - d) % 4) * 16, 16), 16)], 6 + k)
+    for i in range(64):
+        pltpu.make_async_copy(buf.at[1 - core, i], buf.at[1 - core, i], rd.at[i]).wait()
+    for cp in sent:
+        cp.wait_send()
+
+
+def idx_of(me, core):
+    x, y, z = (me // 2) % 4, (me // 8) % 4, me // 32
+    a, c = x + core * (z - x), z + core * (x - z)
+    return c * 16 + y * 4 + a
+
+
+def gather(ms, mt, st):
+    v = pl.BlockSpec(memory_space=pltpu.VMEM)
+    dma = pltpu.SemaphoreType.DMA
+    return pl.pallas_call(
+        gather_kernel,
+        out_shape=(jax.ShapeDtypeStruct((2, 64, 32, 256), BF16), jax.ShapeDtypeStruct((64, 2, 1, 128), F32)),
+        in_specs=[v, v, pl.BlockSpec(memory_space=pltpu.SMEM)], out_specs=(v, v),
+        scratch_shapes=[pltpu.VMEM((2, 16, 256), BF16), pltpu.VMEM((1, 128), F32),
+                        dma((4,)), dma((2,)), dma((9,)), dma((9,)), dma((63,)), dma((64,)), dma((64,)), dma((64,))],
+        compiler_params=pltpu.CompilerParams(collective_id=0, has_side_effects=True),
+    )(ms, mt, st)
+
+
+def sweeps(*args):
     v = pl.BlockSpec(memory_space=pltpu.VMEM)
     return pl.pallas_call(
-        functools.partial(kernel, **kw),
-        out_shape=jax.ShapeDtypeStruct((128, 16, 128), F32),
-        in_specs=[v] * 8, out_specs=v,
+        kernel, out_shape=jax.ShapeDtypeStruct((128, 16, 128), F32), in_specs=[v] * 5, out_specs=v,
         scratch_shapes=[
             pltpu.VMEM((2048, 256), F32), pltpu.VMEM((2048, 256), F32),
-            pltpu.VMEM((16384, 128), BF16), pltpu.VMEM((129, 16, 128), F32)],
-        compiler_params=pltpu.CompilerParams(vmem_limit_bytes=60 * 2**20),
-    )(ms, mt, hs, x0, xr, wi, wo, tri)
-
-
-def triangle():
-    i = jnp.arange(128)
-    same = (i[:, None] % 8) == (i[None, :] % 8)
-    strict = same & ((i[:, None] // 8) < (i[None, :] // 8))
-    t = 256.0 * jnp.concatenate([strict, same], axis=1).astype(F32)
-    return jnp.concatenate([t, t], axis=0).astype(BF16)
+            pltpu.VMEM((16384, 128), BF16), pltpu.VMEM((129, 16, 128), F32),
+            pltpu.VMEM((256, 256), BF16), pltpu.VMEM((16, 256), BF16), pltpu.VMEM((256, 256), BF16)],
+        compiler_params=pltpu.CompilerParams(vmem_limit_bytes=40 * 2**20),
+    )(*args)
+
 
 def untangle(src, out):
     for c in range(10):
@@ -158,20 +324,11 @@
             for k in range(16):
                 out[k, c, 8 * half:8 * half + 8, :] = m[8 * k:8 * k + 8, :]
 
+
 def solution(mesh):
     def local(x_init, w_in, w_out, mod_scale, mod_shift, step_size):
-        me = lax.axis_index("time")
-        half, batch = me // 64, me % 64
-        xr = lax.dynamic_slice(x_init, (batch, half * 8, 0), (1, 8, 10))[0]
-        ms = lax.all_gather(mod_scale, "time", axis=0, tiled=True)
-        mt = lax.all_gather(mod_shift, "time", axis=0, tiled=True)
-        st = lax.all_gather(step_size, "time", axis=0, tiled=True)
-        x0 = jnp.pad(jnp.tile(xr.T, (1, 16)), ((0, 6), (0, 0)))
-        xp = jnp.pad(xr, ((0, 248), (0, 246))).astype(BF16)
-        wi = jnp.pad(w_in, ((0, 246), (0, 0)))
-        wo = jnp.pad(w_out.T, ((0, 6), (0, 0)))
-        hs = jnp.repeat(st * (0.5 / 256.0), 8).reshape(128, 128)
-        mine = call(ms, mt, hs, x0, xp, wi, wo, triangle())
+        buf, hs = gather(mod_scale, mod_shift, step_size)
+        mine = sweeps(buf, hs, jnp.transpose(x_init, (2, 1, 0)), w_in, w_out.T)
         got = lax.all_to_all(mine, "time", 0, 0, tiled=True)
         v = pl.BlockSpec(memory_space=pltpu.VMEM)
         res = pl.pallas_call(untangle, out_shape=jax.ShapeDtypeStruct((16, 10, 16, 64), F32), in_specs=[v], out_specs=v)(got.reshape(2, 64, 16, 128))

time: 215 us -> 99.5 us (0.46)
  blocking collectives: 94 us -> 25.9 us
  waiting for transfers between devices: 58.2 us -> 0 us
  Pallas kernels: 42 us -> 68.5 us
  between operations: 13.5 us -> 0.03 us
    unnamed x1 -> x0, blocking collectives: 69.5 us -> none
    all_gather x2 -> x0, waiting for transfers between devices: 56.8 us -> none  [the longest x1 56.8 us: local(): mt = lax.all_gather(mod_shift, 'time', axis=0, tiled=True)]
    pallas_call x1 -> x2, Pallas kernels: 39.3 us -> 65.8 us  [the longest x1 37.6 us: sweeps(): pl.pallas_call(kernel, out_shape=jax.ShapeDtypeStruct((128, 16, 128), F32...]
    pad x4 -> x0, local copies, waits for them, and re-layouts: 3.91 us -> none  [the longest x1 1.35 us: local(): wi = jnp.pad(w_in, ((0, 246), (0, 0)))]
    unnamed x5 -> x10, local copies, waits for them, and re-layouts: 1.01 us -> 4.7 us
  transfers between devices with their start and end apart: 2 -> 0, of which waited for: 1 -> 0; matrix products, arithmetic and copies ran while one was open for 3% -> 0% of each run, Pallas kernels for 0% -> 0%
where the time goes in v2:
time: 99.5 us; the launch traced here: 99.1 us
  Pallas kernels  68.5 us (69%)
  blocking collectives  25.9 us (26%)
  local copies, waits for them, and re-layouts  4.7 us (5%)
    pallas_call x1, Pallas kernels, sweeps(): pl.pallas_call(kernel, out_shape=jax.ShapeDtypeStruct((128, 16, 128), F32...  37.6 us
    pallas_call x1, Pallas kernels, gather(): pl.pallas_call(gather_kernel, out_shape=(jax.ShapeDtypeStruct((2, 64, 32,...  28.2 us
    all_to_all x1, blocking collectives, local(): got = lax.all_to_all(mine, 'time', 0, 0, tiled=True)  25.9 us
    unnamed x10, local copies, waits for them, and re-layouts  4.7 us
    pallas_call x1, Pallas kernels, local(): pl.pallas_call(untangle, out_shape=jax.ShapeDtypeStruct((16, 10, 16, 64),...  2.73 us

profile of v2, /device:TPU:1, one launch (start us, length us, event | category | flops | bytes accessed | tf_op | source)
XLA Modules:
  0.0 99.1 jit_solution(17842761809937918343)
XLA Ops:
  0.0 28.2 %shard_map.64 = (bf16[2,64,32,256]{3,2,1,0:T(8,128)(2,1)}, f32[64,2,1,128]{3,2,1,0:T(1,128)}) custom-call(bf16[16,256]{1,0:T(8,128)(2,1)} %ms.1, bf16[16,256]{1,0:T(8,128)(2,1)} %mt.1, f32[16]{0:T(128)} %st.1), custom_call_target="tpu_custom_call" | custom-call | tf_op jit(solution)/shard_map/pallas_call | solution.py:298
  28.2 0.0 copy-start
  28.2 1.6 %copy-done = bf16[2,64,32,256]{3,2,1,0:T(8,128)(2,1)S(1)} copy-done((bf16[2,64,32,256]{3,2,1,0:T(8,128)(2,1)S(1)}, bf16[2,64,32,256]{3,2,1,0:T(8,128)(2,1)}, u32[]{:S(2)}) %copy-start) | copy-done | bytes 2097176
  29.8 0.0 copy-start.1
  29.8 0.9 copy-done.1
  30.6 0.0 copy-start.2
  30.6 0.8 copy-done.2
  31.5 0.0 copy-start.3
  31.5 0.7 copy-done.3
  32.2 0.0 copy-start.4
  32.2 0.7 copy-done.4
  32.9 37.6 %shard_map.65 = f32[128,16,128]{2,1,0:T(8,128)S(1)} custom-call(bf16[2,64,32,256]{3,2,1,0:T(8,128)(2,1)S(1)} %copy-done, f32[64,2,1,128]{3,2,1,0:T(1,128)S(1)} %copy-done.2, f32[10,16,64]{2,1,0:T(8,128)S(1)} %bitcast.4, bf16[10,256]{1,0:T(8,128)(2,1)S(1)} %copy-done.3, bf16[10,256]{1,0:T(8,128)(2,1)S(1)} %bitcast.5), custom_call_target="tpu_custom_call" | custom-call | tf_op jit(solution)/shard_map/pallas_call | solution.py:310
  70.5 25.9 %all_to_all.5 = f32[128,16,128]{2,1,0:T(8,128)} all-to-all(f32[128,16,128]{2,1,0:T(8,128)S(1)} %shard_map.65), channel_id=1, replica_groups=mesh['data'=1,'time'=128] {'time'}, dimensions={0} | all-to-all | bytes 2097152 | tf_op jit(solution)/shard_map/all_to_all | solution.py:332
  96.4 2.7 %shard_map.66 = f32[16,10,16,64]{3,2,1,0:T(8,128)} custom-call(f32[2,64,16,128]{3,2,1,0:T(8,128)} %bitcast.6), custom_call_target="tpu_custom_call" | custom-call | tf_op jit(solution)/shard_map/pallas_call | solution.py:334
Async XLA Ops:
  28.2 1.6 %copy-start = (bf16[2,64,32,256]{3,2,1,0:T(8,128)(2,1)S(1)}, bf16[2,64,32,256]{3,2,1,0:T(8,128)(2,1)}, u32[]{:S(2)}) copy-start(bf16[2,64,32,256]{3,2,1,0:T(8,128)(2,1)} %get-tuple-element.7.refs_0_) | copy-start | bytes 6291460
  29.8 0.9 copy-start.1
  30.6 0.8 copy-start.2
  31.5 0.7 copy-start.3
  32.2 0.7 copy-start.4

commit v3 on v2

v3 whole, which is shorter than its diff:
```python
import functools

import jax
import jax.numpy as jnp
from jax import lax
from jax.experimental import pallas as pl
from jax.experimental.pallas import tpu as pltpu
from jax.sharding import PartitionSpec as P

MESH = pl.DeviceIdType.MESH
ROWS = 10
CUBE = 0.044715
ROOT = 0.7978845608028654
F32, BF16 = jnp.float32, jnp.bfloat16

def nn(a, b):
    return lax.dot_general(a, b, (((1,), (0,)), ((), ())), preferred_element_type=F32)

def act(y):
    q = y * ((2.0 * ROOT) + (8.0 * ROOT * CUBE) * (y * y))
    return (y + y * jnp.tanh(q)).astype(BF16)


def gather(ms, mt, st, buf, hs, own, hrow, sx, rx, sh, rh, sm, rm, sd, rd):
    me = lax.axis_index("time")
    core = me % 2
    x, y, z = (me // 2) % 4, (me // 8) % 4, me // 32
    a = x + core * (z - x)
    b = y
    c = z + core * (x - z)
    ka, kc = 1 + 15 * core, 16 - 15 * core

    def dev(da, db, dc):
        aa, bb, cc = (a + da) % 4, (b + db) % 4, (c + dc) % 4
        return 2 * (aa * ka + bb * 4 + cc * kc) + core

    def idx(da, db, dc):
        return ((c + dc) % 4) * 16 + ((b + db) % 4) * 4 + (a + da) % 4

    partner = me + 1 - 2 * core
    peers = [dev(1, 0, 0), dev(3, 0, 0), dev(2, 0, 0), dev(0, 1, 0), dev(0, 3, 0), dev(0, 2, 0),
             dev(0, 0, 1), dev(0, 0, 3), dev(0, 0, 2), partner]
    own[0] = ms[...]
    own[1] = mt[...]
    lane = lax.broadcasted_iota(jnp.int32, (1, 128), 1)
    row = jnp.zeros((1, 128), F32)
    for k in range(16):
        row = jnp.where(lane // 8 == k, st[k] * (0.5 / 256.0), row)
    hrow[...] = row

    barrier = pltpu.get_barrier_semaphore()
    for p in peers:
        pl.semaphore_signal(barrier, inc=1, device_id={"time": p}, device_id_type=MESH)
    pl.semaphore_wait(barrier, len(peers))

    def remote(src, dst, s, r, p):
        cp = pltpu.make_async_remote_copy(src_ref=src, dst_ref=dst, send_sem=s, recv_sem=r,
                                          device_id={"time": p}, device_id_type=MESH)
        cp.start()
        return cp

    mine = idx(0, 0, 0)
    sent = []
    half = pl.ds(pl.multiple_of(core * 16, 16), 16)
    other = pl.ds(pl.multiple_of(16 - core * 16, 16), 16)
    ex = remote(own.at[1 - core], buf.at[1 - core, idx_of(me, 1 - core), half], sx.at[0], rx.at[0], partner)
    hx = remote(hrow, hs.at[idx_of(me, 1 - core), core], sx.at[1], rx.at[1], partner)
    l1 = pltpu.make_async_copy(own.at[core], buf.at[core, mine, half], sx.at[2])
    l2 = pltpu.make_async_copy(hrow, hs.at[mine, core], sx.at[3])
    l1.start(); l2.start()
    ex.wait(); hx.wait(); l1.wait(); l2.wait()

    nsend = [0]
    def send(i, p):
        k = nsend[0]
        nsend[0] += 1
        sent.append(remote(buf.at[core, i], buf.at[core, i], sm.at[k], rm.at[i], p))
    def relay(i, k):
        sent.append(remote(buf.at[core, i], buf.at[core, i], sd.at[k], rd.at[i], partner))
    def arrive(i):
        pltpu.make_async_copy(buf.at[core, i], buf.at[core, i], rm.at[i]).wait()

    hn = [0]
    def hsend(ref, j, p):
        k = hn[0]
        hn[0] += 1
        sent.append(remote(ref, ref, sh.at[k], rh.at[k], p))
    def harrive(ref, k):
        pltpu.make_async_copy(ref, ref, rh.at[k]).wait()

    order = (0, 1, 3, 2)
    for d in order[1:]:
        send(mine, dev(d, 0, 0))
    hm = hs.at[mine]
    for d in order[1:]:
        hsend(hm, d, dev(d, 0, 0))
    relay(mine, 0)
    nrel = 1
    for da in order:
        i = idx(da, 0, 0)
        if da:
            arrive(i)
        for d in order[1:]:
            send(i, dev(0, d, 0))
        for d in (1, 3):
            send(i, dev(0, 0, d))
        if da:
            relay(i, nrel)
            nrel += 1
    for k, d in enumerate(order[1:]):
        harrive(hs.at[idx(-d % 4, 0, 0)], k)
    hb = hs.at[pl.ds(pl.multiple_of(c * 16 + b * 4, 4), 4)]
    for d in order[1:]:
        hsend(hb, d, dev(0, d, 0))
    for db in order[1:]:
        for da in order:
            i = idx(da, db, 0)
            arrive(i)
            for d in (1, 3):
                send(i, dev(0, 0, d))
            relay(i, nrel)
            nrel += 1
    for k, d in enumerate(order[1:]):
        harrive(hs.at[pl.ds(pl.multiple_of(c * 16 + ((b - d) % 4) * 4, 4), 4)], 3 + k)
    hc = hs.at[pl.ds(pl.multiple_of(c * 16, 16), 16)]
    for d in order[1:]:
        hsend(hc, d, dev(0, 0, d))
    n = 0
    for db in order:
        for da in order:
            for dc, step in ((3, 1), (1, 3)):
                i = idx(da, db, dc)
                arrive(i)
                if (n < 8) == (step == 1):
                    send(i, dev(0, 0, step))
                relay(i, nrel)
                nrel += 1
            n += 1
    for db in order:
        for da in order:
            i = idx(da, db, 2)
            arrive(i)
            relay(i, nrel)
            nrel += 1
    for k, d in enumerate(order[1:]):
        harrive(hs.at[pl.ds(pl.multiple_of(((c - d) % 4) * 16, 16), 16)], 6 + k)
    for i in range(64):
        pltpu.make_async_copy(buf.at[1 - core, i], buf.at[1 - core, i], rd.at[i]).wait()
    for cp in sent:
        cp.wait_send()


def idx_of(me, core):
    x, y, z = (me // 2) % 4, (me // 8) % 4, me // 32
    a, c = x + core * (z - x), z + core * (x - z)
    return c * 16 + y * 4 + a


def other(t):
    return (t % 4) * 16 + ((t // 4) % 4) * 4 + t // 16


def body(ms, mt, st, xt_, w_in, w_out, recv, offs, buf, hs, own, hrow, sf, bf, xg, db, wi, wo, tris, sb, tot, ob,
         sx, rx, sh, rh, sm, rm, sd, rd, sa, ra, so, ro, wz, yb, hb, eb):
    gather(ms, mt, st, buf, hs, own, hrow, sx, rx, sh, rh, sm, rm, sd, rd)
    db[128] = jnp.zeros((16, 128), F32)
    me = lax.axis_index("time")
    core = me % 2
    half, batch = me // 64, me % 64
    wi[...] = jnp.zeros_like(wi)
    wo[...] = jnp.zeros_like(wo)
    wi[0:10, :] = w_in[...]
    wo[0:10, :] = w_out[...]
    lane8 = lax.broadcasted_iota(jnp.int32, (8, 128), 1)
    pick = lax.broadcasted_iota(jnp.int32, (8, 64), 1) == batch
    xr = jnp.zeros((8, 128), F32)
    for ch in range(10):
        col = jnp.sum(jnp.where(pick, xt_[ch, pl.ds(pl.multiple_of(half * 8, 8), 8), :], 0.0), axis=1, keepdims=True)
        xr = jnp.where(lane8 == ch, col, xr)
    x0v = jnp.concatenate([xr] * 16, axis=0).T[0:16, :]
    xl = jnp.concatenate([jnp.concatenate([xr, jnp.zeros((8, 128), F32)], axis=0).astype(BF16), jnp.zeros((16, 128), BF16)], axis=1)
    ri = lax.broadcasted_iota(jnp.int32, (256, 256), 0) % 128
    ci = lax.broadcasted_iota(jnp.int32, (256, 256), 1)
    cm = ci % 128
    tri = jnp.where(((ri % 8) == (cm % 8)) & ((ci >= 128) | ((ri // 8) < (cm // 8))), 256.0, 0.0).astype(BF16)
    tris[...] = tri
    u = nn(xl[:, 0:128], wi[...])[:8]
    for k in range(8):
        wz[k] = jnp.zeros((128, 256), BF16)
        wz[k, 16 * k:16 * k + 16, :] = wi[0:16, :]
    wov = wo[...]

    def conv(t, _):
        r = pl.ds(pl.multiple_of(t * 32, 32), 32)
        sf[r, 0, :] = 0.5 + 0.5 * buf[0, t].astype(F32)
        bf[r, 0, :] = 0.5 * buf[1, other(t)].astype(F32)
        return 0
    lax.fori_loop(0, 64, conv, 0)

    def spread(ref, r0):
        return jnp.broadcast_to(ref[pl.ds(r0, 16)], (16, 8, 256)).reshape(128, 256)

    def hidden(g, tau, y):
        r0 = g * 256 + tau * 16
        return act(y * spread(sf, r0) + spread(bf, r0))

    def put(t, d):
        db[2 * t] = d[:, :128]
        db[2 * t + 1] = d[:, 128:]

    def nt(a, b):
        return lax.dot_general(a, b, (((1,), (1,)), ((), ())), preferred_element_type=F32)

    def project(t, h):
        put(t, nt(wov, h))

    def first(g, _):
        uu = jnp.concatenate([u] * 16, axis=0)
        project(lax.rem(8 * g + 63, 64), hb[...])
        for j in range(8):
            h = [hidden(g, 2 * j, uu), hidden(g, 2 * j + 1, uu)]
            h = jnp.concatenate(h, axis=0)
            if j < 7:
                project(8 * g + j, h)
            else:
                hb[...] = h
        return 0

    lane = lax.broadcasted_iota(jnp.int32, (16, 128), 1)
    zb = jnp.zeros((16, 128), BF16)

    def feed(g):
        rolled = None
        prs = []
        for i in range(16):
            t = g * 16 + i
            tile = g * 8 + i // 2
            tile = tile + core * (other(tile) - tile)
            d = db[t]
            here = pltpu.roll(d, 120, 1) if rolled is None else rolled
            rolled = pltpu.roll(db[t + 1], 120, 1)
            gr = (d + jnp.where(lane < 120, here, rolled)) * hs[tile, i % 2]
            hi = gr.astype(BF16)
            r1 = gr - hi.astype(F32)
            mid = r1.astype(BF16)
            lo = (r1 - mid.astype(F32)).astype(BF16)
            prs.append((hi, mid, lo))
        cat = lambda f: jnp.concatenate([f(p) for p in prs], axis=0)
        lhs = jnp.concatenate([cat(lambda p: p[0]), cat(lambda p: p[1])], axis=1)
        eb[...] = nn(lhs, tris[...]) + nn(cat(lambda p: p[2]), tris[0:128, :])

    def drain(carry):
        xs = []
        for i in range(16):
            xs.append(carry + eb[16 * i:16 * i + 16, :128])
            carry = carry + eb[16 * i:16 * i + 16, 128:]
        return xs, carry

    def store_x(g, xs):
        for q in range(2):
            xg[2 * g + q] = jnp.concatenate(xs[8 * q:8 * q + 8], axis=0).astype(BF16).T

    def lift(g, tau):
        return nn(xg[2 * g + tau // 8], wz[tau % 8])

    def drift(g, n):
        project(lax.rem(8 * g + 63, 64), hb[...])
        y = {k: yb[k] for k in range(3)}
        h = []
        for tau in range(16):
            if tau < 13:
                y[tau + 3] = lift(g, tau + 3)
            h += [hidden(g, tau, y[tau])]
            if tau >= 13:
                yb[tau - 13] = lift(n, tau - 13)
            if tau == 15:
                hb[...] = jnp.concatenate(h, axis=0)
            elif tau % 2:
                project(8 * g + tau // 2, jnp.concatenate(h, axis=0))
                h = []

    def later(i, carry):
        g = lax.rem(i, 8)
        n = lax.rem(i + 1, 8)
        carry = jnp.where(n == 0, x0v, carry)
        xs, carry = drain(carry)
        store_x(n, xs)
        feed(lax.rem(i + 2, 8))
        drift(g, n)
        return carry

    hb[...] = jnp.zeros_like(hb)
    lax.fori_loop(0, 8, first, 0)
    project(63, hb[...])
    feed(0)
    xs, carry = drain(x0v)
    store_x(0, xs)
    feed(1)
    for tau in range(3):
        yb[tau] = lift(0, tau)
    carry = lax.fori_loop(0, 16, later, carry)
    project(63, hb[...])

    def scan(g, carry):
        feed(g)
        xs, carry = drain(carry)
        store_x(g, xs)
        return carry
    lax.fori_loop(0, 8, scan, x0v)
    g0 = me % 8

    def collect(g):
        for i in range(16):
            sb[16 * g + i] = eb[16 * i:16 * i + 16, :128]
            tot[16 * g + i] = eb[16 * i:16 * i + 16, 128:]

    def ship(g):
        for i in range(16):
            q = 16 * g + i

            @pl.when(q != me)
            def _():
                bulk(q).start()

    def bulk(q):
        return pltpu.make_async_remote_copy(src_ref=sb.at[q, pl.ds(0, ROWS)], dst_ref=recv.at[me, pl.ds(0, ROWS)], send_sem=sa.at[q],
                                            recv_sem=ra.at[me], device_id={"time": q}, device_id_type=MESH)

    def last(drains, feeds):
        def run(i, _):
            g = lax.rem(g0 + i, 8)
            if drains:
                collect(lax.rem(g + 5, 8))
            if feeds:
                feed(lax.rem(g + 6, 8))
            drift(g, lax.rem(g + 1, 8))
            if drains:
                ship(lax.rem(g + 5, 8))
            return 0
        return run
    for tau in range(3):
        yb[tau] = lift(g0, tau)
    lax.fori_loop(0, 2, last(False, False), 0)
    last(False, True)(2, 0)
    lax.fori_loop(3, 8, last(True, True), 0)
    project(lax.rem(8 * g0 + 63, 64), hb[...])
    collect(lax.rem(g0 + 5, 8))
    feed(lax.rem(g0 + 6, 8))
    ship(lax.rem(g0 + 5, 8))
    collect(lax.rem(g0 + 6, 8))
    feed(lax.rem(g0 + 7, 8))
    ship(lax.rem(g0 + 6, 8))
    collect(lax.rem(g0 + 7, 8))

    diag = lane // 8 == lax.broadcasted_iota(jnp.int32, (16, 128), 0)

    def offsets(g, carry):
        for i in range(16):
            ob[16 * g + i] = jnp.sum(jnp.where(diag, carry, 0.0), axis=0, keepdims=True)
            carry = carry + tot[16 * g + i]
        return carry
    lax.fori_loop(0, 8, offsets, x0v)
    ship(lax.rem(g0 + 7, 8))

    def small(q):
        return pltpu.make_async_remote_copy(src_ref=ob.at[q], dst_ref=offs.at[me], send_sem=so.at[q],
                                            recv_sem=ro.at[me], device_id={"time": q}, device_id_type=MESH)

    def post(k, _):
        small(lax.rem(me + k, 128)).start()
        return 0
    lax.fori_loop(1, 128, post, 0)
    recv[me] = sb[me]
    offs[me] = ob[me]

    def settle(k, _):
        q = lax.rem(me + k, 128)
        bulk(q).wait_send()
        small(q).wait_send()
        pltpu.make_async_copy(recv.at[q, pl.ds(0, ROWS)], recv.at[q, pl.ds(0, ROWS)], ra.at[q]).wait()
        pltpu.make_async_copy(offs.at[q], offs.at[q], ro.at[q]).wait()
        return 0
    lax.fori_loop(1, 128, settle, 0)


def sweeps(*args):
    v = pl.BlockSpec(memory_space=pltpu.VMEM)
    dma = pltpu.SemaphoreType.DMA
    return pl.pallas_call(
        body,
        out_shape=(jax.ShapeDtypeStruct((128, 16, 128), F32), jax.ShapeDtypeStruct((128, 1, 128), F32)),
        in_specs=[v, v, pl.BlockSpec(memory_space=pltpu.SMEM), v, v, v], out_specs=(v, v),
        scratch_shapes=[
            pltpu.VMEM((2, 64, 32, 256), BF16), pltpu.VMEM((64, 2, 1, 128), F32),
            pltpu.VMEM((2, 16, 256), BF16), pltpu.VMEM((1, 128), F32),
            pltpu.VMEM((2048, 1, 256), F32), pltpu.VMEM((2048, 1, 256), F32),
            pltpu.VMEM((16, 128, 128), BF16), pltpu.VMEM((129, 16, 128), F32),
            pltpu.VMEM((128, 256), BF16), pltpu.VMEM((16, 256), BF16), pltpu.VMEM((256, 256), BF16),
            pltpu.VMEM((128, 16, 128), F32), pltpu.VMEM((128, 16, 128), F32), pltpu.VMEM((128, 1, 128), F32),
            dma((4,)), dma((2,)), dma((9,)), dma((9,)), dma((63,)), dma((64,)), dma((64,)), dma((64,)),
            dma((128,)), dma((128,)), dma((128,)), dma((128,)),
            pltpu.VMEM((8, 128, 256), BF16), pltpu.VMEM((3, 128, 256), F32), pltpu.VMEM((256, 256), BF16), pltpu.VMEM((256, 256), F32)],
        compiler_params=pltpu.CompilerParams(vmem_limit_bytes=40 * 2**20, collective_id=0, has_side_effects=True),
    )(*args)


def untangle(src, off, out):
    for half in range(2):
        base = off[64 * half:64 * half + 64, :].T
        for c in range(10):
            m = src[half, :, c, :].T
            for k in range(16):
                out[k, c, 8 * half:8 * half + 8, :] = m[8 * k:8 * k + 8, :] + base[8 * c:8 * c + 8, :]


def solution(mesh):
    def local(x_init, w_in, w_out, mod_scale, mod_shift, step_size):
        got, off = sweeps(mod_scale, mod_shift, step_size, jnp.transpose(x_init, (2, 1, 0)), w_in, w_out.T)
        v = pl.BlockSpec(memory_space=pltpu.VMEM)
        res = pl.pallas_call(untangle, out_shape=jax.ShapeDtypeStruct((16, 10, 16, 64), F32), in_specs=[v, v], out_specs=v)(
            got.reshape(2, 64, 16, 128), off.reshape(128, 128))
        return jnp.transpose(res, (0, 3, 2, 1))

    return jax.shard_map(local, mesh=mesh, in_specs=(P("data"), P(), P(), P("time"), P("time"), P("time")), out_specs=P("time", "data"), check_vma=False)
```

time: 99.5 us -> 87.7 us (0.88)
  blocking collectives: 25.9 us -> 0 us
  Pallas kernels: 68.5 us -> 81.4 us
  local copies, waits for them, and re-layouts: 4.7 us -> 5.91 us
    all_to_all x1 -> x0, blocking collectives: 25.9 us -> none  [local(): got = lax.all_to_all(mine, 'time', 0, 0, tiled=True)]
    pallas_call x2 -> x1, Pallas kernels: 65.8 us -> 78.7 us  [sweeps(): pl.pallas_call(body, out_shape=(jax.ShapeDtypeStruct((128, 16, 128), F32)...]
    unnamed x10 -> x16, local copies, waits for them, and re-layouts: 4.7 us -> 5.91 us
where the time goes in v3:
time: 87.7 us; the launch traced here: 87.3 us
  Pallas kernels  81.4 us (93%)
  local copies, waits for them, and re-layouts  5.91 us (7%)
    pallas_call x1, Pallas kernels, sweeps(): pl.pallas_call(body, out_shape=(jax.ShapeDtypeStruct((128, 16, 128), F32)...  78.7 us
    unnamed x16, local copies, waits for them, and re-layouts  5.91 us
    pallas_call x1, Pallas kernels, local(): pl.pallas_call(untangle, out_shape=jax.ShapeDtypeStruct((16, 10, 16, 64),...  2.73 us

profile of v3, /device:TPU:1, one launch (start us, length us, event | category | flops | bytes accessed | tf_op | source)
XLA Modules:
  0.0 87.3 jit_solution(16875291396837497633)
XLA Ops:
  0.0 0.0 copy-start.1
  0.0 0.9 %copy-done.1 = f32[64,16,10]{0,1,2:T(8,128)S(1)} copy-done((f32[64,16,10]{0,1,2:T(8,128)S(1)}, f32[64,16,10]{0,1,2:T(8,128)}, u32[]{:S(2)}) %copy-start.1) | copy-done | bytes 40984
  0.9 0.0 copy-start.3
  0.9 0.7 copy-done.3
  1.6 0.0 copy-start.4
  1.6 0.7 copy-done.4
  2.3 0.0 copy-start.5
  2.3 0.7 copy-done.5
  3.0 0.0 copy-start.6
  3.0 0.7 copy-done.6
  3.7 0.0 copy-start.7
  3.7 0.7 copy-done.7
  4.3 78.7 %shard_map.64 = (f32[128,16,128]{2,1,0:T(8,128)S(1)}, f32[128,1,128]{2,1,0:T(1,128)S(1)}) custom-call(bf16[16,256]{1,0:T(8,128)(2,1)S(1)} %copy-done.3, bf16[16,256]{1,0:T(8,128)(2,1)S(1)} %copy-done.4, f32[16]{0:T(128)S(1)} %copy-done.7, f32[10,16,64]{2,1,0:T(8,128)S(1)} %bitcast.6, bf16[10,256]{1,0:T(8,128)(2,1)S(1)} %copy-done.5, bf16[10,256]{1,0:T(8,128)(2,1)S(1)} %bitcast.8), custom_call_target="tpu_custom_call" | custom-call | tf_op jit(solution)/shard_map/pallas_call | solution.py:389
  83.0 0.0 copy-start
  83.0 1.0 %copy-done = f32[128,16,128]{2,1,0:T(8,128)} copy-done((f32[128,16,128]{2,1,0:T(8,128)}, f32[128,16,128]{2,1,0:T(8,128)S(1)}, u32[]{:S(2)}) %copy-start) | copy-done | bytes 1048600
  84.0 0.0 copy-start.2
  84.0 0.6 copy-done.2
  84.6 2.7 %shard_map.65 = f32[16,10,16,64]{3,2,1,0:T(8,128)} custom-call(f32[2,64,16,128]{3,2,1,0:T(8,128)} %bitcast.5, f32[128,128]{1,0:T(8,128)} %bitcast.7), custom_call_target="tpu_custom_call" | custom-call | tf_op jit(solution)/shard_map/pallas_call | solution.py:420
Async XLA Ops:
  0.0 0.9 %copy-start.1 = (f32[64,16,10]{0,1,2:T(8,128)S(1)}, f32[64,16,10]{0,1,2:T(8,128)}, u32[]{:S(2)}) copy-start(f32[64,16,10]{0,1,2:T(8,128)} %param.6) | copy-start | bytes 122884
  0.9 0.7 copy-start.3
  1.6 0.7 copy-start.4
  2.3 0.7 copy-start.5
  3.0 0.7 copy-start.6
  3.7 0.7 copy-start.7
  83.0 1.0 %copy-start = (f32[128,16,128]{2,1,0:T(8,128)}, f32[128,16,128]{2,1,0:T(8,128)S(1)}, u32[]{:S(2)}) copy-start(f32[128,16,128]{2,1,0:T(8,128)S(1)} %get-tuple-element.7) | copy-start | bytes 3145732
  84.0 0.6 copy-start.2

commit v4 on v3

--- a/solution.py
+++ b/solution.py
@@ -21,148 +21,108 @@
     return (y + y * jnp.tanh(q)).astype(BF16)
 
 
-def gather(ms, mt, st, buf, hs, own, hrow, sx, rx, sh, rh, sm, rm, sd, rd):
+def coords(me):
+    return (me // 2) % 4, (me // 8) % 4, me // 32
+
+
+def gather(ms, mt, st, buf, hs, sl, ss, sh, rab, rc, rf, rd, rh):
     me = lax.axis_index("time")
     core = me % 2
-    x, y, z = (me // 2) % 4, (me // 8) % 4, me // 32
+    x, y, z = coords(me)
     a = x + core * (z - x)
     b = y
     c = z + core * (x - z)
     ka, kc = 1 + 15 * core, 16 - 15 * core
+    base = core * 64
 
     def dev(da, db, dc):
         aa, bb, cc = (a + da) % 4, (b + db) % 4, (c + dc) % 4
         return 2 * (aa * ka + bb * 4 + cc * kc) + core
 
-    def idx(da, db, dc):
-        return ((c + dc) % 4) * 16 + ((b + db) % 4) * 4 + (a + da) % 4
+    def group(db, dc):
+        return pl.ds(pl.multiple_of(base + ((c + dc) % 4) * 16 + ((b + db) % 4) * 4, 4), 4)
 
     partner = me + 1 - 2 * core
-    peers = [dev(1, 0, 0), dev(3, 0, 0), dev(2, 0, 0), dev(0, 1, 0), dev(0, 3, 0), dev(0, 2, 0),
-             dev(0, 0, 1), dev(0, 0, 3), dev(0, 0, 2), partner]
-    own[0] = ms[...]
-    own[1] = mt[...]
+    mine = base + c * 16 + b * 4 + a
+    plane = [(da, db) for db in (0, 1, 3, 2) for da in (0, 1, 3, 2) if da or db]
+    peers = [dev(da, db, 0) for da, db in plane] + [dev(0, 0, 1), dev(0, 0, 3), dev(0, 0, 2), partner]
+
+    barrier = pltpu.get_barrier_semaphore()
+    for p in peers:
+        pl.semaphore_signal(barrier, inc=1, device_id={"time": p}, device_id_type=MESH)
+    loads = [pltpu.make_async_copy(ms, buf.at[mine, 0], sl.at[0]), pltpu.make_async_copy(mt, buf.at[mine, 1], sl.at[1])]
+    for cp in loads:
+        cp.start()
     lane = lax.broadcasted_iota(jnp.int32, (1, 128), 1)
     row = jnp.zeros((1, 128), F32)
     for k in range(16):
         row = jnp.where(lane // 8 == k, st[k] * (0.5 / 256.0), row)
-    hrow[...] = row
-
-    barrier = pltpu.get_barrier_semaphore()
-    for p in peers:
-        pl.semaphore_signal(barrier, inc=1, device_id={"time": p}, device_id_type=MESH)
+    hs[mine] = row
+    for cp in loads:
+        cp.wait()
     pl.semaphore_wait(barrier, len(peers))
 
-    def remote(src, dst, s, r, p):
-        cp = pltpu.make_async_remote_copy(src_ref=src, dst_ref=dst, send_sem=s, recv_sem=r,
-                                          device_id={"time": p}, device_id_type=MESH)
-        cp.start()
-        return cp
-
-    mine = idx(0, 0, 0)
-    sent = []
-    half = pl.ds(pl.multiple_of(core * 16, 16), 16)
-    other = pl.ds(pl.multiple_of(16 - core * 16, 16), 16)
-    ex = remote(own.at[1 - core], buf.at[1 - core, idx_of(me, 1 - core), half], sx.at[0], rx.at[0], partner)
-    hx = remote(hrow, hs.at[idx_of(me, 1 - core), core], sx.at[1], rx.at[1], partner)
-    l1 = pltpu.make_async_copy(own.at[core], buf.at[core, mine, half], sx.at[2])
-    l2 = pltpu.make_async_copy(hrow, hs.at[mine, core], sx.at[3])
-    l1.start(); l2.start()
-    ex.wait(); hx.wait(); l1.wait(); l2.wait()
-
-    nsend = [0]
-    def send(i, p):
-        k = nsend[0]
-        nsend[0] += 1
-        sent.append(remote(buf.at[core, i], buf.at[core, i], sm.at[k], rm.at[i], p))
-    def relay(i, k):
-        sent.append(remote(buf.at[core, i], buf.at[core, i], sd.at[k], rd.at[i], partner))
-    def arrive(i):
-        pltpu.make_async_copy(buf.at[core, i], buf.at[core, i], rm.at[i]).wait()
-
-    hn = [0]
-    def hsend(ref, j, p):
-        k = hn[0]
-        hn[0] += 1
-        sent.append(remote(ref, ref, sh.at[k], rh.at[k], p))
-    def harrive(ref, k):
-        pltpu.make_async_copy(ref, ref, rh.at[k]).wait()
-
+    def send(ref, s, r, p):
+        pltpu.make_async_remote_copy(src_ref=ref, dst_ref=ref, send_sem=s, recv_sem=r,
+                                     device_id={"time": p}, device_id_type=MESH).start()
+
+    def arrive(ref, r):
+        pltpu.make_async_copy(ref, ref, r).wait()
+
+    for da, db in plane:
+        send(buf.at[mine], ss, rab.at[db], dev(da, db, 0))
+    for da, db in plane:
+        send(hs.at[mine], sh, rh.at[0], dev(da, db, 0))
     order = (0, 1, 3, 2)
-    for d in order[1:]:
-        send(mine, dev(d, 0, 0))
-    hm = hs.at[mine]
-    for d in order[1:]:
-        hsend(hm, d, dev(d, 0, 0))
-    relay(mine, 0)
-    nrel = 1
-    for da in order:
-        i = idx(da, 0, 0)
-        if da:
-            arrive(i)
-        for d in order[1:]:
-            send(i, dev(0, d, 0))
-        for d in (1, 3):
-            send(i, dev(0, 0, d))
-        if da:
-            relay(i, nrel)
-            nrel += 1
-    for k, d in enumerate(order[1:]):
-        harrive(hs.at[idx(-d % 4, 0, 0)], k)
-    hb = hs.at[pl.ds(pl.multiple_of(c * 16 + b * 4, 4), 4)]
-    for d in order[1:]:
-        hsend(hb, d, dev(0, d, 0))
-    for db in order[1:]:
-        for da in order:
-            i = idx(da, db, 0)
-            arrive(i)
-            for d in (1, 3):
-                send(i, dev(0, 0, d))
-            relay(i, nrel)
-            nrel += 1
-    for k, d in enumerate(order[1:]):
-        harrive(hs.at[pl.ds(pl.multiple_of(c * 16 + ((b - d) % 4) * 4, 4), 4)], 3 + k)
-    hc = hs.at[pl.ds(pl.multiple_of(c * 16, 16), 16)]
-    for d in order[1:]:
-        hsend(hc, d, dev(0, 0, d))
-    n = 0
     for db in order:
-        for da in order:
-            for dc, step in ((3, 1), (1, 3)):
-                i = idx(da, db, dc)
-                arrive(i)
-                if (n < 8) == (step == 1):
-                    send(i, dev(0, 0, step))
-                relay(i, nrel)
-                nrel += 1
-            n += 1
+        ref = buf.at[group(4 - db, 0)]
+        if db:
+            arrive(ref, rab.at[db])
+        else:
+            arrive(buf.at[pl.ds(0, 3)], rab.at[0])
+        send(ref, ss, rc.at[0, db], dev(0, 0, 1))
+        send(ref, ss, rc.at[1, db], dev(0, 0, 3))
+        send(ref, ss, rd.at[0], partner)
+    arrive(hs.at[pl.ds(0, 15)], rh.at[0])
+    rows = hs.at[pl.ds(pl.multiple_of(base + c * 16, 16), 16)]
+    for d in (1, 3, 2):
+        send(rows, sh, rh.at[1], dev(0, 0, d))
+    for n, db in enumerate(order):
+        up = buf.at[group(4 - db, 3)]
+        arrive(up, rc.at[0, db])
+        if n < 2:
+            send(up, ss, rf.at[db], dev(0, 0, 1))
+        send(up, ss, rd.at[1], partner)
+        down = buf.at[group(4 - db, 1)]
+        arrive(down, rc.at[1, db])
+        if n >= 2:
+            send(down, ss, rf.at[db], dev(0, 0, 3))
+        send(down, ss, rd.at[2], partner)
+    arrive(hs.at[pl.ds(0, 48)], rh.at[1])
+    send(hs.at[pl.ds(pl.multiple_of(base, 64), 64)], sh, rh.at[2], partner)
     for db in order:
-        for da in order:
-            i = idx(da, db, 2)
-            arrive(i)
-            relay(i, nrel)
-            nrel += 1
-    for k, d in enumerate(order[1:]):
-        harrive(hs.at[pl.ds(pl.multiple_of(((c - d) % 4) * 16, 16), 16)], 6 + k)
-    for i in range(64):
-        pltpu.make_async_copy(buf.at[1 - core, i], buf.at[1 - core, i], rd.at[i]).wait()
-    for cp in sent:
-        cp.wait_send()
-
-
-def idx_of(me, core):
-    x, y, z = (me // 2) % 4, (me // 8) % 4, me // 32
-    a, c = x + core * (z - x), z + core * (x - z)
-    return c * 16 + y * 4 + a
+        far = buf.at[group(4 - db, 2)]
+        arrive(far, rf.at[db])
+        send(far, ss, rd.at[3], partner)
+    for k in range(4):
+        arrive(buf.at[pl.ds(0, 16)], rd.at[k])
+    arrive(hs.at[pl.ds(0, 64)], rh.at[2])
+    arrive(buf.at[pl.ds(0, 127)], ss)
+    arrive(hs.at[pl.ds(0, 127)], sh)
 
 
 def other(t):
     return (t % 4) * 16 + ((t // 4) % 4) * 4 + t // 16
 
 
-def body(ms, mt, st, xt_, w_in, w_out, recv, offs, buf, hs, own, hrow, sf, bf, xg, db, wi, wo, tris, sb, tot, ob,
-         sx, rx, sh, rh, sm, rm, sd, rd, sa, ra, so, ro, wz, yb, hb, eb):
-    gather(ms, mt, st, buf, hs, own, hrow, sx, rx, sh, rh, sm, rm, sd, rd)
+def body(ms, mt, st, xh, wih, woh, recv, offs, buf, hs, xt_, w_in, w_out, sf, bf, xg, db, wi, wo, tris, sb, tot, ob,
+         sl, ss, sh, rab, rc, rf, rd, rh, sa, wz, yb, hb, eb):
+    early = [pltpu.make_async_copy(*pair, sl.at[2 + k]) for k, pair in enumerate(((xh, xt_), (wih, w_in), (woh, w_out)))]
+    for cp in early:
+        cp.start()
+    gather(ms, mt, st, buf, hs, sl, ss, sh, rab, rc, rf, rd, rh)
+    for cp in early:
+        cp.wait()
     db[128] = jnp.zeros((16, 128), F32)
     me = lax.axis_index("time")
     core = me % 2
@@ -191,9 +151,10 @@
     wov = wo[...]
 
     def conv(t, _):
-        r = pl.ds(pl.multiple_of(t * 32, 32), 32)
-        sf[r, 0, :] = 0.5 + 0.5 * buf[0, t].astype(F32)
-        bf[r, 0, :] = 0.5 * buf[1, other(t)].astype(F32)
+        for q, n in ((0, t), (1, 64 + other(t))):
+            r = pl.ds(t * 32 + 16 * q, 16)
+            sf[r, 0, :] = 0.5 + 0.5 * buf[n, 0].astype(F32)
+            bf[r, 0, :] = 0.5 * buf[n, 1].astype(F32)
         return 0
     lax.fori_loop(0, 64, conv, 0)
 
@@ -235,11 +196,11 @@
         for i in range(16):
             t = g * 16 + i
             tile = g * 8 + i // 2
-            tile = tile + core * (other(tile) - tile)
+            tile = 64 + other(tile) if i % 2 else tile
             d = db[t]
             here = pltpu.roll(d, 120, 1) if rolled is None else rolled
             rolled = pltpu.roll(db[t + 1], 120, 1)
-            gr = (d + jnp.where(lane < 120, here, rolled)) * hs[tile, i % 2]
+            gr = (d + jnp.where(lane < 120, here, rolled)) * hs[tile]
             hi = gr.astype(BF16)
             r1 = gr - hi.astype(F32)
             mid = r1.astype(BF16)
@@ -323,8 +284,8 @@
                 bulk(q).start()
 
     def bulk(q):
-        return pltpu.make_async_remote_copy(src_ref=sb.at[q, pl.ds(0, ROWS)], dst_ref=recv.at[me, pl.ds(0, ROWS)], send_sem=sa.at[q],
-                                            recv_sem=ra.at[me], device_id={"time": q}, device_id_type=MESH)
+        return pltpu.make_async_remote_copy(src_ref=sb.at[q, pl.ds(0, ROWS)], dst_ref=recv.at[me, pl.ds(0, ROWS)], send_sem=sa.at[0],
+                                            recv_sem=sa.at[1], device_id={"time": q}, device_id_type=MESH)
 
     def last(drains, feeds):
         def run(i, _):
@@ -363,8 +324,8 @@
     ship(lax.rem(g0 + 7, 8))
 
     def small(q):
-        return pltpu.make_async_remote_copy(src_ref=ob.at[q], dst_ref=offs.at[me], send_sem=so.at[q],
-                                            recv_sem=ro.at[me], device_id={"time": q}, device_id_type=MESH)
+        return pltpu.make_async_remote_copy(src_ref=ob.at[q], dst_ref=offs.at[me], send_sem=sa.at[2],
+                                            recv_sem=sa.at[3], device_id={"time": q}, device_id_type=MESH)
 
     def post(k, _):
         small(lax.rem(me + k, 128)).start()
@@ -373,34 +334,29 @@
     recv[me] = sb[me]
     offs[me] = ob[me]
 
-    def settle(k, _):
-        q = lax.rem(me + k, 128)
-        bulk(q).wait_send()
-        small(q).wait_send()
-        pltpu.make_async_copy(recv.at[q, pl.ds(0, ROWS)], recv.at[q, pl.ds(0, ROWS)], ra.at[q]).wait()
-        pltpu.make_async_copy(offs.at[q], offs.at[q], ro.at[q]).wait()
-        return 0
-    lax.fori_loop(1, 128, settle, 0)
+    for k, ref in enumerate((sb.at[pl.ds(0, 127), pl.ds(0, ROWS)], recv.at[pl.ds(0, 127), pl.ds(0, ROWS)],
+                             ob.at[pl.ds(0, 127)], offs.at[pl.ds(0, 127)])):
+        pltpu.make_async_copy(ref, ref, sa.at[k]).wait()
 
 
 def sweeps(*args):
     v = pl.BlockSpec(memory_space=pltpu.VMEM)
+    h = pl.BlockSpec(memory_space=pltpu.HBM)
     dma = pltpu.SemaphoreType.DMA
     return pl.pallas_call(
         body,
         out_shape=(jax.ShapeDtypeStruct((128, 16, 128), F32), jax.ShapeDtypeStruct((128, 1, 128), F32)),
-        in_specs=[v, v, pl.BlockSpec(memory_space=pltpu.SMEM), v, v, v], out_specs=(v, v),
+        in_specs=[h, h, pl.BlockSpec(memory_space=pltpu.SMEM), h, h, h], out_specs=(v, v),
         scratch_shapes=[
-            pltpu.VMEM((2, 64, 32, 256), BF16), pltpu.VMEM((64, 2, 1, 128), F32),
-            pltpu.VMEM((2, 16, 256), BF16), pltpu.VMEM((1, 128), F32),
+            pltpu.VMEM((128, 2, 16, 256), BF16), pltpu.VMEM((128, 1, 128), F32),
+            pltpu.VMEM((10, 16, 64), F32), pltpu.VMEM((10, 256), BF16), pltpu.VMEM((10, 256), BF16),
             pltpu.VMEM((2048, 1, 256), F32), pltpu.VMEM((2048, 1, 256), F32),
             pltpu.VMEM((16, 128, 128), BF16), pltpu.VMEM((129, 16, 128), F32),
             pltpu.VMEM((128, 256), BF16), pltpu.VMEM((16, 256), BF16), pltpu.VMEM((256, 256), BF16),
             pltpu.VMEM((128, 16, 128), F32), pltpu.VMEM((128, 16, 128), F32), pltpu.VMEM((128, 1, 128), F32),
-            dma((4,)), dma((2,)), dma((9,)), dma((9,)), dma((63,)), dma((64,)), dma((64,)), dma((64,)),
-            dma((128,)), dma((128,)), dma((128,)), dma((128,)),
+            dma((5,)), dma, dma, dma((4,)), dma((2, 4)), dma((4,)), dma((4,)), dma((3,)), dma((4,)),
             pltpu.VMEM((8, 128, 256), BF16), pltpu.VMEM((3, 128, 256), F32), pltpu.VMEM((256, 256), BF16), pltpu.VMEM((256, 256), F32)],
-        compiler_params=pltpu.CompilerParams(vmem_limit_bytes=40 * 2**20, collective_id=0, has_side_effects=True),
+        compiler_params=pltpu.CompilerParams(vmem_limit_bytes=58 * 2**20, collective_id=0, has_side_effects=True),
     )(*args)
 
 

time: 87.7 us -> 74.8 us (0.85)
  Pallas kernels: 81.4 us -> 74.6 us
  local copies, waits for them, and re-layouts: 5.91 us -> 0 us
    pallas_call x1, Pallas kernels: 78.7 us -> 71.9 us  [sweeps(): pl.pallas_call(body, out_shape=(jax.ShapeDtypeStruct((128, 16, 128), F32)...]
    unnamed x16 -> x0, local copies, waits for them, and re-layouts: 5.91 us -> none
where the time goes in v4:
time: 74.8 us; the launch traced here: 74.6 us
  Pallas kernels  74.6 us (100%)
    pallas_call x1, Pallas kernels, sweeps(): pl.pallas_call(body, out_shape=(jax.ShapeDtypeStruct((128, 16, 128), F32)...  71.9 us
    pallas_call x1, Pallas kernels, local(): pl.pallas_call(untangle, out_shape=jax.ShapeDtypeStruct((16, 10, 16, 64),...  2.73 us

profile of v4, /device:TPU:1, one launch (start us, length us, event | category | flops | bytes accessed | tf_op | source)
XLA Modules:
  0.0 74.6 jit_solution(16451012906933938785)
XLA Ops:
  0.0 71.9 %shard_map.64 = (f32[128,16,128]{2,1,0:T(8,128)}, f32[128,1,128]{2,1,0:T(1,128)}) custom-call(bf16[16,256]{1,0:T(8,128)(2,1)} %ms.1, bf16[16,256]{1,0:T(8,128)(2,1)} %mt.1, f32[16]{0:T(128)} %st.1, f32[10,16,64]{2,1,0:T(8,128)} %bitcast.6, bf16[10,256]{1,0:T(8,128)(2,1)} %wih.1, bf16[10,256]{1,0:T(8,128)(2,1)} %bitcast.8), custom_call_target="tpu_custom_call" | custom-call | tf_op jit(solution)/shard_map/pallas_call | solution.py:346
  71.9 2.7 %shard_map.65 = f32[16,10,16,64]{3,2,1,0:T(8,128)} custom-call(f32[2,64,16,128]{3,2,1,0:T(8,128)} %bitcast.5, f32[128,128]{1,0:T(8,128)} %bitcast.7), custom_call_target="tpu_custom_call" | custom-call | tf_op jit(solution)/shard_map/pallas_call | solution.py:376

commit v5 on v4

--- a/solution.py
+++ b/solution.py
@@ -9,6 +9,7 @@
 
 MESH = pl.DeviceIdType.MESH
 ROWS = 10
+FEED = 9
 CUBE = 0.044715
 ROOT = 0.7978845608028654
 F32, BF16 = jnp.float32, jnp.bfloat16
@@ -25,7 +26,7 @@
     return (me // 2) % 4, (me // 8) % 4, me // 32
 
 
-def gather(ms, mt, st, buf, hs, sl, ss, sh, rab, rc, rf, rd, rh):
+def gather(ms, mt, st, buf, hs, sl, ss, sh, rab, rc, rf, rd, rh, ready, work):
     me = lax.axis_index("time")
     core = me % 2
     x, y, z = coords(me)
@@ -73,6 +74,7 @@
         send(buf.at[mine], ss, rab.at[db], dev(da, db, 0))
     for da, db in plane:
         send(hs.at[mine], sh, rh.at[0], dev(da, db, 0))
+    ready()
     order = (0, 1, 3, 2)
     for db in order:
         ref = buf.at[group(4 - db, 0)]
@@ -87,6 +89,19 @@
     rows = hs.at[pl.ds(pl.multiple_of(base + c * 16, 16), 16)]
     for d in (1, 3, 2):
         send(rows, sh, rh.at[1], dev(0, 0, d))
+
+    def run(db, dc):
+        return base + ((c + dc) % 4) * 16 + ((b + db) % 4) * 4
+
+    pc = x + core * (z - x)
+    pbase = 64 - base
+
+    def prun(k, dc):
+        return pbase + ((pc + dc) % 4) * 16 + 4 * k
+
+    work([run(k, 0) for k in range(4)])
+    arrive(buf.at[pl.ds(0, 16)], rd.at[0])
+    work([prun(k, 0) for k in range(4)])
     for n, db in enumerate(order):
         up = buf.at[group(4 - db, 3)]
         arrive(up, rc.at[0, db])
@@ -98,14 +113,22 @@
         if n >= 2:
             send(down, ss, rf.at[db], dev(0, 0, 3))
         send(down, ss, rd.at[2], partner)
+        if n < 3:
+            work([run(4 - db, 3), run(4 - db, 1)])
     arrive(hs.at[pl.ds(0, 48)], rh.at[1])
     send(hs.at[pl.ds(pl.multiple_of(base, 64), 64)], sh, rh.at[2], partner)
     for db in order:
         far = buf.at[group(4 - db, 2)]
         arrive(far, rf.at[db])
         send(far, ss, rd.at[3], partner)
-    for k in range(4):
-        arrive(buf.at[pl.ds(0, 16)], rd.at[k])
+    work([run(4 - order[3], 3), run(4 - order[3], 1)])
+    arrive(buf.at[pl.ds(0, 16)], rd.at[1])
+    work([prun(k, 3) for k in range(4)])
+    arrive(buf.at[pl.ds(0, 16)], rd.at[2])
+    work([prun(k, 1) for k in range(4)])
+    work([run(k, 2) for k in range(4)])
+    arrive(buf.at[pl.ds(0, 16)], rd.at[3])
+    work([prun(k, 2) for k in range(4)])
     arrive(hs.at[pl.ds(0, 64)], rh.at[2])
     arrive(buf.at[pl.ds(0, 127)], ss)
     arrive(hs.at[pl.ds(0, 127)], sh)
@@ -116,47 +139,38 @@
 
 
 def body(ms, mt, st, xh, wih, woh, recv, offs, buf, hs, xt_, w_in, w_out, sf, bf, xg, db, wi, wo, tris, sb, tot, ob,
-         sl, ss, sh, rab, rc, rf, rd, rh, sa, wz, yb, hb, eb):
+         sl, ss, sh, rab, rc, rf, rd, rh, sa, wz, yb, hb, eb, ub, x0s):
     early = [pltpu.make_async_copy(*pair, sl.at[2 + k]) for k, pair in enumerate(((xh, xt_), (wih, w_in), (woh, w_out)))]
     for cp in early:
         cp.start()
-    gather(ms, mt, st, buf, hs, sl, ss, sh, rab, rc, rf, rd, rh)
-    for cp in early:
-        cp.wait()
     db[128] = jnp.zeros((16, 128), F32)
     me = lax.axis_index("time")
     core = me % 2
     half, batch = me // 64, me % 64
-    wi[...] = jnp.zeros_like(wi)
-    wo[...] = jnp.zeros_like(wo)
-    wi[0:10, :] = w_in[...]
-    wo[0:10, :] = w_out[...]
-    lane8 = lax.broadcasted_iota(jnp.int32, (8, 128), 1)
-    pick = lax.broadcasted_iota(jnp.int32, (8, 64), 1) == batch
-    xr = jnp.zeros((8, 128), F32)
-    for ch in range(10):
-        col = jnp.sum(jnp.where(pick, xt_[ch, pl.ds(pl.multiple_of(half * 8, 8), 8), :], 0.0), axis=1, keepdims=True)
-        xr = jnp.where(lane8 == ch, col, xr)
-    x0v = jnp.concatenate([xr] * 16, axis=0).T[0:16, :]
-    xl = jnp.concatenate([jnp.concatenate([xr, jnp.zeros((8, 128), F32)], axis=0).astype(BF16), jnp.zeros((16, 128), BF16)], axis=1)
-    ri = lax.broadcasted_iota(jnp.int32, (256, 256), 0) % 128
-    ci = lax.broadcasted_iota(jnp.int32, (256, 256), 1)
-    cm = ci % 128
-    tri = jnp.where(((ri % 8) == (cm % 8)) & ((ci >= 128) | ((ri // 8) < (cm // 8))), 256.0, 0.0).astype(BF16)
-    tris[...] = tri
-    u = nn(xl[:, 0:128], wi[...])[:8]
-    for k in range(8):
-        wz[k] = jnp.zeros((128, 256), BF16)
-        wz[k, 16 * k:16 * k + 16, :] = wi[0:16, :]
-    wov = wo[...]
-
-    def conv(t, _):
-        for q, n in ((0, t), (1, 64 + other(t))):
-            r = pl.ds(t * 32 + 16 * q, 16)
-            sf[r, 0, :] = 0.5 + 0.5 * buf[n, 0].astype(F32)
-            bf[r, 0, :] = 0.5 * buf[n, 1].astype(F32)
-        return 0
-    lax.fori_loop(0, 64, conv, 0)
+    def prepare():
+        wi[...] = jnp.zeros_like(wi)
+        wo[...] = jnp.zeros_like(wo)
+        wi[0:10, :] = w_in[...]
+        wo[0:10, :] = w_out[...]
+        lane8 = lax.broadcasted_iota(jnp.int32, (8, 128), 1)
+        pick = lax.broadcasted_iota(jnp.int32, (8, 64), 1) == batch
+        xr = jnp.zeros((8, 128), F32)
+        for ch in range(10):
+            col = jnp.sum(jnp.where(pick, xt_[ch, pl.ds(pl.multiple_of(half * 8, 8), 8), :], 0.0), axis=1, keepdims=True)
+            xr = jnp.where(lane8 == ch, col, xr)
+        x0v = jnp.concatenate([xr] * 16, axis=0).T[0:16, :]
+        xl = jnp.concatenate([jnp.concatenate([xr, jnp.zeros((8, 128), F32)], axis=0).astype(BF16), jnp.zeros((16, 128), BF16)], axis=1)
+        ri = lax.broadcasted_iota(jnp.int32, (256, 256), 0) % 128
+        ci = lax.broadcasted_iota(jnp.int32, (256, 256), 1)
+        cm = ci % 128
+        tri = jnp.where(((ri % 8) == (cm % 8)) & ((ci >= 128) | ((ri // 8) < (cm // 8))), 256.0, 0.0).astype(BF16)
+        tris[...] = tri
+        u = nn(xl[:, 0:128], wi[...])[:8]
+        for k in range(8):
+            wz[k] = jnp.zeros((128, 256), BF16)
+            wz[k, 16 * k:16 * k + 16, :] = wi[0:16, :]
+        x0s[...] = x0v
+        ub[...] = jnp.concatenate([u] * 16, axis=0)
 
     def spread(ref, r0):
         return jnp.broadcast_to(ref[pl.ds(r0, 16)], (16, 8, 256)).reshape(128, 256)
@@ -175,17 +189,29 @@
     def project(t, h):
         put(t, nt(wov, h))
 
-    def first(g, _):
-        uu = jnp.concatenate([u] * 16, axis=0)
-        project(lax.rem(8 * g + 63, 64), hb[...])
-        for j in range(8):
-            h = [hidden(g, 2 * j, uu), hidden(g, 2 * j + 1, uu)]
-            h = jnp.concatenate(h, axis=0)
-            if j < 7:
-                project(8 * g + j, h)
-            else:
-                hb[...] = h
-        return 0
+    def ready():
+        for cp in early:
+            cp.wait()
+        prepare()
+
+    def work(runs):
+        uu = ub[...]
+        h = []
+        blocks = [(n + k, k) for n in runs for k in range(4)]
+        for q, (n, _) in enumerate(blocks):
+            tree = n // 64
+            idx = n - 64 * tree
+            t = 2 * (idx + tree * (other(idx) - idx)) + tree
+            r = pl.ds(t * 16, 16)
+            sf[r, 0, :] = 0.5 + 0.5 * buf[n, 0].astype(F32)
+            bf[r, 0, :] = 0.5 * buf[n, 1].astype(F32)
+            h.append(act(uu * spread(sf, t * 16) + spread(bf, t * 16)))
+            if q % 2:
+                d = nt(wo[...], jnp.concatenate(h, axis=0))
+                db[tp] = d[:, :128]
+                db[t] = d[:, 128:]
+                h = []
+            tp = t
 
     lane = lax.broadcasted_iota(jnp.int32, (16, 128), 1)
     zb = jnp.zeros((16, 128), BF16)
@@ -224,16 +250,18 @@
     def lift(g, tau):
         return nn(xg[2 * g + tau // 8], wz[tau % 8])
 
-    def drift(g, n):
+    def drift(g, n, hooks={}):
         project(lax.rem(8 * g + 63, 64), hb[...])
         y = {k: yb[k] for k in range(3)}
         h = []
         for tau in range(16):
             if tau < 13:
                 y[tau + 3] = lift(g, tau + 3)
+            if 11 <= tau < 14:
+                yb[tau - 11] = lift(n, tau - 11)
             h += [hidden(g, tau, y[tau])]
-            if tau >= 13:
-                yb[tau - 13] = lift(n, tau - 13)
+            if tau in hooks:
+                hooks[tau]()
             if tau == 15:
                 hb[...] = jnp.concatenate(h, axis=0)
             elif tau % 2:
@@ -250,9 +278,10 @@
         drift(g, n)
         return carry
 
+    gather(ms, mt, st, buf, hs, sl, ss, sh, rab, rc, rf, rd, rh, ready, work)
+    x0v = x0s[...]
+    wov = wo[...]
     hb[...] = jnp.zeros_like(hb)
-    lax.fori_loop(0, 8, first, 0)
-    project(63, hb[...])
     feed(0)
     xs, carry = drain(x0v)
     store_x(0, xs)
@@ -287,30 +316,27 @@
         return pltpu.make_async_remote_copy(src_ref=sb.at[q, pl.ds(0, ROWS)], dst_ref=recv.at[me, pl.ds(0, ROWS)], send_sem=sa.at[0],
                                             recv_sem=sa.at[1], device_id={"time": q}, device_id_type=MESH)
 
-    def last(drains, feeds):
+    def last(feeds, ships):
         def run(i, _):
             g = lax.rem(g0 + i, 8)
-            if drains:
-                collect(lax.rem(g + 5, 8))
+            hooks = {}
+            if ships:
+                hooks[2] = lambda: ship(lax.rem(g + 6, 8))
             if feeds:
-                feed(lax.rem(g + 6, 8))
-            drift(g, lax.rem(g + 1, 8))
-            if drains:
-                ship(lax.rem(g + 5, 8))
+                hooks[FEED] = lambda: feed(lax.rem(g + 7, 8))
+            drift(g, lax.rem(g + 1, 8), hooks)
+            if feeds:
+                collect(lax.rem(g + 7, 8))
             return 0
         return run
     for tau in range(3):
         yb[tau] = lift(g0, tau)
-    lax.fori_loop(0, 2, last(False, False), 0)
-    last(False, True)(2, 0)
-    lax.fori_loop(3, 8, last(True, True), 0)
+    last(False, False)(0, 0)
+    last(True, False)(1, 0)
+    lax.fori_loop(2, 8, last(True, True), 0)
     project(lax.rem(8 * g0 + 63, 64), hb[...])
-    collect(lax.rem(g0 + 5, 8))
-    feed(lax.rem(g0 + 6, 8))
-    ship(lax.rem(g0 + 5, 8))
-    collect(lax.rem(g0 + 6, 8))
+    ship(lax.rem(g0 + 6, 8))
     feed(lax.rem(g0 + 7, 8))
-    ship(lax.rem(g0 + 6, 8))
     collect(lax.rem(g0 + 7, 8))
 
     diag = lane // 8 == lax.broadcasted_iota(jnp.int32, (16, 128), 0)
@@ -355,7 +381,8 @@
             pltpu.VMEM((128, 256), BF16), pltpu.VMEM((16, 256), BF16), pltpu.VMEM((256, 256), BF16),
             pltpu.VMEM((128, 16, 128), F32), pltpu.VMEM((128, 16, 128), F32), pltpu.VMEM((128, 1, 128), F32),
             dma((5,)), dma, dma, dma((4,)), dma((2, 4)), dma((4,)), dma((4,)), dma((3,)), dma((4,)),
-            pltpu.VMEM((8, 128, 256), BF16), pltpu.VMEM((3, 128, 256), F32), pltpu.VMEM((256, 256), BF16), pltpu.VMEM((256, 256), F32)],
+            pltpu.VMEM((8, 128, 256), BF16), pltpu.VMEM((3, 128, 256), F32), pltpu.VMEM((256, 256), BF16), pltpu.VMEM((256, 256), F32),
+            pltpu.VMEM((128, 256), F32), pltpu.VMEM((16, 128), F32)],
         compiler_params=pltpu.CompilerParams(vmem_limit_bytes=58 * 2**20, collective_id=0, has_side_effects=True),
     )(*args)
 

time: 74.8 us -> 66.5 us (0.89)
  Pallas kernels: 74.6 us -> 66.3 us
    pallas_call x1, Pallas kernels: 71.9 us -> 63.6 us  [sweeps(): pl.pallas_call(body, out_shape=(jax.ShapeDtypeStruct((128, 16, 128), F32)...]
where the time goes in v5:
time: 66.5 us; the launch traced here: 66.3 us
  Pallas kernels  66.3 us (100%)
    pallas_call x1, Pallas kernels, sweeps(): pl.pallas_call(body, out_shape=(jax.ShapeDtypeStruct((128, 16, 128), F32)...  63.6 us
    pallas_call x1, Pallas kernels, local(): pl.pallas_call(untangle, out_shape=jax.ShapeDtypeStruct((16, 10, 16, 64),...  2.73 us

profile of v5, /device:TPU:1, one launch (start us, length us, event | category | flops | bytes accessed | tf_op | source)
XLA Modules:
  0.0 66.3 jit_solution(8017555161808641186)
XLA Ops:
  0.0 63.6 %shard_map.64 = (f32[128,16,128]{2,1,0:T(8,128)}, f32[128,1,128]{2,1,0:T(1,128)}) custom-call(bf16[16,256]{1,0:T(8,128)(2,1)} %ms.1, bf16[16,256]{1,0:T(8,128)(2,1)} %mt.1, f32[16]{0:T(128)} %st.1, f32[10,16,64]{2,1,0:T(8,128)} %bitcast.6, bf16[10,256]{1,0:T(8,128)(2,1)} %wih.1, bf16[10,256]{1,0:T(8,128)(2,1)} %bitcast.8), custom_call_target="tpu_custom_call" | custom-call | tf_op jit(solution)/shard_map/pallas_call | solution.py:372
  63.6 2.7 %shard_map.65 = f32[16,10,16,64]{3,2,1,0:T(8,128)} custom-call(f32[2,64,16,128]{3,2,1,0:T(8,128)} %bitcast.5, f32[128,128]{1,0:T(8,128)} %bitcast.7), custom_call_target="tpu_custom_call" | custom-call | tf_op jit(solution)/shard_map/pallas_call | solution.py:403

commit v6 on v5

--- a/solution.py
+++ b/solution.py
@@ -26,7 +26,7 @@
     return (me // 2) % 4, (me // 8) % 4, me // 32
 
 
-def gather(ms, mt, st, buf, hs, sl, ss, sh, rab, rc, rf, rd, rh, ready, work):
+def gather(ms, mt, st, buf, hs, sl, ss, sh, rab, rc, rf, rd, rp, rh, ready, work):
     me = lax.axis_index("time")
     core = me % 2
     x, y, z = coords(me)
@@ -75,6 +75,9 @@
     for da, db in plane:
         send(hs.at[mine], sh, rh.at[0], dev(da, db, 0))
     ready()
+    def run(db, dc):
+        return base + ((c + dc) % 4) * 16 + ((b + db) % 4) * 4
+
     order = (0, 1, 3, 2)
     for db in order:
         ref = buf.at[group(4 - db, 0)]
@@ -85,49 +88,49 @@
         send(ref, ss, rc.at[0, db], dev(0, 0, 1))
         send(ref, ss, rc.at[1, db], dev(0, 0, 3))
         send(ref, ss, rd.at[0], partner)
+        if db != 2:
+            work([run(4 - db, 0)])
     arrive(hs.at[pl.ds(0, 15)], rh.at[0])
     rows = hs.at[pl.ds(pl.multiple_of(base + c * 16, 16), 16)]
     for d in (1, 3, 2):
         send(rows, sh, rh.at[1], dev(0, 0, d))
 
-    def run(db, dc):
-        return base + ((c + dc) % 4) * 16 + ((b + db) % 4) * 4
-
     pc = x + core * (z - x)
     pbase = 64 - base
 
     def prun(k, dc):
         return pbase + ((pc + dc) % 4) * 16 + 4 * k
 
-    work([run(k, 0) for k in range(4)])
+    work([run(2, 0)])
     arrive(buf.at[pl.ds(0, 16)], rd.at[0])
     work([prun(k, 0) for k in range(4)])
+    def theirs(n):
+        for k in range(2):
+            arrive(buf.at[pl.ds(0, 4)], rp.at[k, n])
+        q = ((b + 4 - order[n]) % 4)
+        return [prun(q, 3), prun(q, 1)]
+
     for n, db in enumerate(order):
         up = buf.at[group(4 - db, 3)]
         arrive(up, rc.at[0, db])
         if n < 2:
             send(up, ss, rf.at[db], dev(0, 0, 1))
-        send(up, ss, rd.at[1], partner)
+        send(up, ss, rp.at[0, n], partner)
         down = buf.at[group(4 - db, 1)]
         arrive(down, rc.at[1, db])
         if n >= 2:
             send(down, ss, rf.at[db], dev(0, 0, 3))
-        send(down, ss, rd.at[2], partner)
+        send(down, ss, rp.at[1, n], partner)
         if n < 3:
-            work([run(4 - db, 3), run(4 - db, 1)])
+            work([run(4 - db, 3), run(4 - db, 1)] + (theirs(n - 1) if n else []))
     arrive(hs.at[pl.ds(0, 48)], rh.at[1])
     send(hs.at[pl.ds(pl.multiple_of(base, 64), 64)], sh, rh.at[2], partner)
     for db in order:
         far = buf.at[group(4 - db, 2)]
         arrive(far, rf.at[db])
-        send(far, ss, rd.at[3], partner)
-    work([run(4 - order[3], 3), run(4 - order[3], 1)])
+        send(far, ss, rd.at[1], partner)
+    work([run(4 - order[3], 3), run(4 - order[3], 1)] + theirs(2) + [run(k, 2) for k in range(4)] + theirs(3))
     arrive(buf.at[pl.ds(0, 16)], rd.at[1])
-    work([prun(k, 3) for k in range(4)])
-    arrive(buf.at[pl.ds(0, 16)], rd.at[2])
-    work([prun(k, 1) for k in range(4)])
-    work([run(k, 2) for k in range(4)])
-    arrive(buf.at[pl.ds(0, 16)], rd.at[3])
     work([prun(k, 2) for k in range(4)])
     arrive(hs.at[pl.ds(0, 64)], rh.at[2])
     arrive(buf.at[pl.ds(0, 127)], ss)
@@ -139,7 +142,7 @@
 
 
 def body(ms, mt, st, xh, wih, woh, recv, offs, buf, hs, xt_, w_in, w_out, sf, bf, xg, db, wi, wo, tris, sb, tot, ob,
-         sl, ss, sh, rab, rc, rf, rd, rh, sa, wz, yb, hb, eb, ub, x0s):
+         sl, ss, sh, rab, rc, rf, rd, rp, rh, sa, wz, yb, hb, eb, eb2, ub, x0s):
     early = [pltpu.make_async_copy(*pair, sl.at[2 + k]) for k, pair in enumerate(((xh, xt_), (wih, w_in), (woh, w_out)))]
     for cp in early:
         cp.start()
@@ -216,7 +219,8 @@
     lane = lax.broadcasted_iota(jnp.int32, (16, 128), 1)
     zb = jnp.zeros((16, 128), BF16)
 
-    def feed(g):
+    def feed(g, e=None):
+        e = eb if e is None else e
         rolled = None
         prs = []
         for i in range(16):
@@ -234,13 +238,14 @@
             prs.append((hi, mid, lo))
         cat = lambda f: jnp.concatenate([f(p) for p in prs], axis=0)
         lhs = jnp.concatenate([cat(lambda p: p[0]), cat(lambda p: p[1])], axis=1)
-        eb[...] = nn(lhs, tris[...]) + nn(cat(lambda p: p[2]), tris[0:128, :])
-
-    def drain(carry):
+        e[...] = nn(lhs, tris[...]) + nn(cat(lambda p: p[2]), tris[0:128, :])
+
+    def drain(carry, e=None):
+        e = eb if e is None else e
         xs = []
         for i in range(16):
-            xs.append(carry + eb[16 * i:16 * i + 16, :128])
-            carry = carry + eb[16 * i:16 * i + 16, 128:]
+            xs.append(carry + e[16 * i:16 * i + 16, :128])
+            carry = carry + e[16 * i:16 * i + 16, 128:]
         return xs, carry
 
     def store_x(g, xs):
@@ -278,7 +283,7 @@
         drift(g, n)
         return carry
 
-    gather(ms, mt, st, buf, hs, sl, ss, sh, rab, rc, rf, rd, rh, ready, work)
+    gather(ms, mt, st, buf, hs, sl, ss, sh, rab, rc, rf, rd, rp, rh, ready, work)
     x0v = x0s[...]
     wov = wo[...]
     hb[...] = jnp.zeros_like(hb)
@@ -291,18 +296,25 @@
     carry = lax.fori_loop(0, 16, later, carry)
     project(63, hb[...])
 
-    def scan(g, carry):
-        feed(g)
-        xs, carry = drain(carry)
-        store_x(g, xs)
+    def scan(k, carry):
+        for e, f, g in ((eb, eb2, 2 * k), (eb2, eb, 2 * k + 1)):
+            xs, carry = drain(carry, e)
+            feed(lax.rem(g + 1, 8), f)
+            store_x(g, xs)
         return carry
-    lax.fori_loop(0, 8, scan, x0v)
+    feed(0)
+    lax.fori_loop(0, 4, scan, x0v)
     g0 = me % 8
+
+    diag = lane // 8 == lax.broadcasted_iota(jnp.int32, (16, 128), 0)
+
+    def strip(v):
+        return jnp.sum(jnp.where(diag, v, 0.0), axis=0, keepdims=True)
 
     def collect(g):
         for i in range(16):
             sb[16 * g + i] = eb[16 * i:16 * i + 16, :128]
-            tot[16 * g + i] = eb[16 * i:16 * i + 16, 128:]
+            tot[16 * g + i] = strip(eb[16 * i:16 * i + 16, 128:])
 
     def ship(g):
         for i in range(16):
@@ -339,14 +351,12 @@
     feed(lax.rem(g0 + 7, 8))
     collect(lax.rem(g0 + 7, 8))
 
-    diag = lane // 8 == lax.broadcasted_iota(jnp.int32, (16, 128), 0)
-
     def offsets(g, carry):
         for i in range(16):
-            ob[16 * g + i] = jnp.sum(jnp.where(diag, carry, 0.0), axis=0, keepdims=True)
+            ob[16 * g + i] = carry
             carry = carry + tot[16 * g + i]
         return carry
-    lax.fori_loop(0, 8, offsets, x0v)
+    lax.fori_loop(0, 8, offsets, strip(x0v))
     ship(lax.rem(g0 + 7, 8))
 
     def small(q):
@@ -379,9 +389,9 @@
             pltpu.VMEM((2048, 1, 256), F32), pltpu.VMEM((2048, 1, 256), F32),
             pltpu.VMEM((16, 128, 128), BF16), pltpu.VMEM((129, 16, 128), F32),
             pltpu.VMEM((128, 256), BF16), pltpu.VMEM((16, 256), BF16), pltpu.VMEM((256, 256), BF16),
-            pltpu.VMEM((128, 16, 128), F32), pltpu.VMEM((128, 16, 128), F32), pltpu.VMEM((128, 1, 128), F32),
-            dma((5,)), dma, dma, dma((4,)), dma((2, 4)), dma((4,)), dma((4,)), dma((3,)), dma((4,)),
-            pltpu.VMEM((8, 128, 256), BF16), pltpu.VMEM((3, 128, 256), F32), pltpu.VMEM((256, 256), BF16), pltpu.VMEM((256, 256), F32),
+            pltpu.VMEM((128, 16, 128), F32), pltpu.VMEM((128, 1, 128), F32), pltpu.VMEM((128, 1, 128), F32),
+            dma((5,)), dma, dma, dma((4,)), dma((2, 4)), dma((4,)), dma((2,)), dma((2, 4)), dma((3,)), dma((4,)),
+            pltpu.VMEM((8, 128, 256), BF16), pltpu.VMEM((3, 128, 256), F32), pltpu.VMEM((256, 256), BF16), pltpu.VMEM((256, 256), F32), pltpu.VMEM((256, 256), F32),
             pltpu.VMEM((128, 256), F32), pltpu.VMEM((16, 128), F32)],
         compiler_params=pltpu.CompilerParams(vmem_limit_bytes=58 * 2**20, collective_id=0, has_side_effects=True),
     )(*args)

time: 66.5 us -> 65.1 us (0.979)
  Pallas kernels: 66.3 us -> 64.9 us
    pallas_call x1, Pallas kernels: 63.6 us -> 62.1 us  [sweeps(): pl.pallas_call(body, out_shape=(jax.ShapeDtypeStruct((128, 16, 128), F32)...]
where the time goes in v6:
time: 65.1 us; the launch traced here: 64.9 us
  Pallas kernels  64.9 us (100%)
    pallas_call x1, Pallas kernels, sweeps(): pl.pallas_call(body, out_shape=(jax.ShapeDtypeStruct((128, 16, 128), F32)...  62.1 us
    pallas_call x1, Pallas kernels, local(): pl.pallas_call(untangle, out_shape=jax.ShapeDtypeStruct((16, 10, 16, 64),...  2.73 us

profile of v6, /device:TPU:1, one launch (start us, length us, event | category | flops | bytes accessed | tf_op | source)
XLA Modules:
  0.0 64.9 jit_solution(8929276181333654430)
XLA Ops:
  0.0 62.1 %shard_map.64 = (f32[128,16,128]{2,1,0:T(8,128)}, f32[128,1,128]{2,1,0:T(1,128)}) custom-call(bf16[16,256]{1,0:T(8,128)(2,1)} %ms.1, bf16[16,256]{1,0:T(8,128)(2,1)} %mt.1, f32[16]{0:T(128)} %st.1, f32[10,16,64]{2,1,0:T(8,128)} %bitcast.6, bf16[10,256]{1,0:T(8,128)(2,1)} %wih.1, bf16[10,256]{1,0:T(8,128)(2,1)} %bitcast.8), custom_call_target="tpu_custom_call" | custom-call | tf_op jit(solution)/shard_map/pallas_call | solution.py:382
  62.2 2.7 %shard_map.65 = f32[16,10,16,64]{3,2,1,0:T(8,128)} custom-call(f32[2,64,16,128]{3,2,1,0:T(8,128)} %bitcast.5, f32[128,128]{1,0:T(8,128)} %bitcast.7), custom_call_target="tpu_custom_call" | custom-call | tf_op jit(solution)/shard_map/pallas_call | solution.py:413

commit v7 on v6

--- a/solution.py
+++ b/solution.py
@@ -26,7 +26,7 @@
     return (me // 2) % 4, (me // 8) % 4, me // 32
 
 
-def gather(ms, mt, st, buf, hs, sl, ss, sh, rab, rc, rf, rd, rp, rh, ready, work):
+def gather(ms, mt, st, sv, buf, hs, sl, ss, sh, rab, rc, rf, rd, rp, rh, ready, work):
     me = lax.axis_index("time")
     core = me % 2
     x, y, z = coords(me)
@@ -51,16 +51,17 @@
     barrier = pltpu.get_barrier_semaphore()
     for p in peers:
         pl.semaphore_signal(barrier, inc=1, device_id={"time": p}, device_id_type=MESH)
-    loads = [pltpu.make_async_copy(ms, buf.at[mine, 0], sl.at[0]), pltpu.make_async_copy(mt, buf.at[mine, 1], sl.at[1])]
+    loads = [pltpu.make_async_copy(ms, buf.at[mine, 0], sl.at[0]), pltpu.make_async_copy(mt, buf.at[mine, 1], sl.at[1]),
+             pltpu.make_async_copy(st, sv, sl.at[5])]
     for cp in loads:
         cp.start()
+    for cp in loads:
+        cp.wait()
     lane = lax.broadcasted_iota(jnp.int32, (1, 128), 1)
     row = jnp.zeros((1, 128), F32)
     for k in range(16):
-        row = jnp.where(lane // 8 == k, st[k] * (0.5 / 256.0), row)
+        row = jnp.where(lane // 8 == k, sv[0:1, k:k + 1] * (0.5 / 256.0), row)
     hs[mine] = row
-    for cp in loads:
-        cp.wait()
     pl.semaphore_wait(barrier, len(peers))
 
     def send(ref, s, r, p):
@@ -142,7 +143,7 @@
 
 
 def body(ms, mt, st, xh, wih, woh, recv, offs, buf, hs, xt_, w_in, w_out, sf, bf, xg, db, wi, wo, tris, sb, tot, ob,
-         sl, ss, sh, rab, rc, rf, rd, rp, rh, sa, wz, yb, hb, eb, eb2, ub, x0s):
+         sl, ss, sh, rab, rc, rf, rd, rp, rh, sa, wz, yb, hb, eb, eb2, ub, x0s, sv):
     early = [pltpu.make_async_copy(*pair, sl.at[2 + k]) for k, pair in enumerate(((xh, xt_), (wih, w_in), (woh, w_out)))]
     for cp in early:
         cp.start()
@@ -283,7 +284,7 @@
         drift(g, n)
         return carry
 
-    gather(ms, mt, st, buf, hs, sl, ss, sh, rab, rc, rf, rd, rp, rh, ready, work)
+    gather(ms, mt, st, sv, buf, hs, sl, ss, sh, rab, rc, rf, rd, rp, rh, ready, work)
     x0v = x0s[...]
     wov = wo[...]
     hb[...] = jnp.zeros_like(hb)
@@ -382,7 +383,7 @@
     return pl.pallas_call(
         body,
         out_shape=(jax.ShapeDtypeStruct((128, 16, 128), F32), jax.ShapeDtypeStruct((128, 1, 128), F32)),
-        in_specs=[h, h, pl.BlockSpec(memory_space=pltpu.SMEM), h, h, h], out_specs=(v, v),
+        in_specs=[h] * 6, out_specs=(v, v),
         scratch_shapes=[
             pltpu.VMEM((128, 2, 16, 256), BF16), pltpu.VMEM((128, 1, 128), F32),
             pltpu.VMEM((10, 16, 64), F32), pltpu.VMEM((10, 256), BF16), pltpu.VMEM((10, 256), BF16),
@@ -390,9 +391,9 @@
             pltpu.VMEM((16, 128, 128), BF16), pltpu.VMEM((129, 16, 128), F32),
             pltpu.VMEM((128, 256), BF16), pltpu.VMEM((16, 256), BF16), pltpu.VMEM((256, 256), BF16),
             pltpu.VMEM((128, 16, 128), F32), pltpu.VMEM((128, 1, 128), F32), pltpu.VMEM((128, 1, 128), F32),
-            dma((5,)), dma, dma, dma((4,)), dma((2, 4)), dma((4,)), dma((2,)), dma((2, 4)), dma((3,)), dma((4,)),
+            dma((6,)), dma, dma, dma((4,)), dma((2, 4)), dma((4,)), dma((2,)), dma((2, 4)), dma((3,)), dma((4,)),
             pltpu.VMEM((8, 128, 256), BF16), pltpu.VMEM((3, 128, 256), F32), pltpu.VMEM((256, 256), BF16), pltpu.VMEM((256, 256), F32), pltpu.VMEM((256, 256), F32),
-            pltpu.VMEM((128, 256), F32), pltpu.VMEM((16, 128), F32)],
+            pltpu.VMEM((128, 256), F32), pltpu.VMEM((16, 128), F32), pltpu.VMEM((1, 16), F32)],
         compiler_params=pltpu.CompilerParams(vmem_limit_bytes=58 * 2**20, collective_id=0, has_side_effects=True),
     )(*args)
 
@@ -408,7 +409,7 @@
 
 def solution(mesh):
     def local(x_init, w_in, w_out, mod_scale, mod_shift, step_size):
-        got, off = sweeps(mod_scale, mod_shift, step_size, jnp.transpose(x_init, (2, 1, 0)), w_in, w_out.T)
+        got, off = sweeps(mod_scale, mod_shift, step_size.reshape(1, 16), jnp.transpose(x_init, (2, 1, 0)), w_in, w_out.T)
         v = pl.BlockSpec(memory_space=pltpu.VMEM)
         res = pl.pallas_call(untangle, out_shape=jax.ShapeDtypeStruct((16, 10, 16, 64), F32), in_specs=[v, v], out_specs=v)(
             got.reshape(2, 64, 16, 128), off.reshape(128, 128))

time: 65.1 us -> 64.3 us (0.988)
  Pallas kernels: 64.9 us -> 64.1 us
    pallas_call x1, Pallas kernels: 62.1 us -> 61.4 us  [sweeps(): pl.pallas_call(body, out_shape=(jax.ShapeDtypeStruct((128, 16, 128), F32)...]
where the time goes in v7:
time: 64.3 us; the launch traced here: 64.1 us
  Pallas kernels  64.1 us (100%)
    pallas_call x1, Pallas kernels, sweeps(): pl.pallas_call(body, out_shape=(jax.ShapeDtypeStruct((128, 16, 128), F32)...  61.4 us
    pallas_call x1, Pallas kernels, local(): pl.pallas_call(untangle, out_shape=jax.ShapeDtypeStruct((16, 10, 16, 64),...  2.73 us

profile of v7, /device:TPU:1, one launch (start us, length us, event | category | flops | bytes accessed | tf_op | source)
XLA Modules:
  0.0 64.1 jit_solution(13523267147226308141)
XLA Ops:
  0.0 61.4 %shard_map.64 = (f32[128,16,128]{2,1,0:T(8,128)}, f32[128,1,128]{2,1,0:T(1,128)}) custom-call(bf16[16,256]{1,0:T(8,128)(2,1)} %ms.1, bf16[16,256]{1,0:T(8,128)(2,1)} %mt.1, f32[1,16]{1,0:T(1,128)} %bitcast.10, f32[10,16,64]{2,1,0:T(8,128)} %bitcast.7, bf16[10,256]{1,0:T(8,128)(2,1)} %wih.1, bf16[10,256]{1,0:T(8,128)(2,1)} %bitcast.9), custom_call_target="tpu_custom_call" | custom-call | tf_op jit(solution)/shard_map/pallas_call | solution.py:383
  61.4 2.7 %shard_map.65 = f32[16,10,16,64]{3,2,1,0:T(8,128)} custom-call(f32[2,64,16,128]{3,2,1,0:T(8,128)} %bitcast.6, f32[128,128]{1,0:T(8,128)} %bitcast.8), custom_call_target="tpu_custom_call" | custom-call | tf_op jit(solution)/shard_map/pallas_call | solution.py:414
